TPU v7x, 32 devices: a whole 2x2x4 slice. The times are simulated.
32 devices in a mesh: seq: 4 (over y, x), batch: 8 (over z, core).
Axes of the slice: x: 2, y: 2, z: 4, core: 2. Of those that a mesh axis runs over, the one named last changes fastest.
Arguments:
- attn_out: bfloat16 [16384, 2560], P(('seq', 'batch')), may hold values from -200 to 200
- out_grad: bfloat16 [16384, 2560], P(('seq', 'batch')), may hold values from -6 to 6
- master: float32 [2560, 2560], P(('seq', 'batch')), may hold values from -0.125 to 0.125
- moment_one: float32 [2560, 2560], P(('seq', 'batch')), may hold values from -4 to 4
- moment_two: float32 [2560, 2560], P(('seq', 'batch')), may hold values from 0.002 to 0.05
Outputs:
- input_grad: bfloat16 [16384, 2560], P(('seq', 'batch'))
- new_master: float32 [2560, 2560], P(('seq', 'batch'))
- new_moment_one: float32 [2560, 2560], P(('seq', 'batch'))
- new_moment_two: float32 [2560, 2560], P(('seq', 'batch'))
All inputs are finite; a program needn't handle non-finite values.
Results may differ from a plain program's by a relative error of at most 0.01.
Values may be sent and summed in bfloat16 or wider, within the bound.
A program may use at most 128 MiB of HBM per device.

v0:
```python
import functools
import jax
import jax.numpy as jnp
from jax import lax
from jax.experimental import pallas as pl
from jax.experimental.pallas import tpu as pltpu
from jax.sharding import PartitionSpec as P

GRAD_BLOCKS = 4
STEP = 10
MESH = pl.DeviceIdType.MESH
F32 = jnp.float32
BF16 = jnp.bfloat16


def kernel(nb, attn_hbm, og_hbm, w_ref, ig_ref, gw_ref, sq_ref,
           attn_ref, og_ref, l_s, rx_attn, rx_og, tbuf, attn_t, wg, g, r1a, r1b, r2, t2, pz, rz, sqs,
           x_s, x_r, z_s, z_r, p_s, p_r, d_s, d_r, c_s, c_r,
           s1_s, s1_r, s2_s, s2_r, rz_s, rz_r, q_s, q_r):
    ns = 4
    nz = nb // 2
    tok, din = attn_ref.shape
    dout = og_ref.shape[1]
    r = w_ref.shape[0]
    half = dout // 2
    block = nb * r
    seq = lax.axis_index("seq")
    batch = lax.axis_index("batch")
    z = batch // 2
    core = batch % 2
    hi = seq // 2
    lo = seq % 2
    sh = (1 - hi) * 2 + lo
    sl = hi * 2 + (1 - lo)
    sd = (1 - hi) * 2 + (1 - lo)
    hi_dev = (sh, batch)
    lo_dev = (sl, batch)
    core_dev = (seq, z * 2 + 1 - core)
    cols_a = pl.ds(0, half)
    cols_b = pl.ds(half, half)

    def other(i):
        f = lax.rem(seq * nb + batch + i, ns * nb)
        return (f // nb, lax.rem(f, nb))

    la = pltpu.make_async_copy(attn_hbm, attn_ref, l_s.at[0])
    la.start()
    lg = pltpu.make_async_copy(og_hbm, og_ref, l_s.at[1])
    lg.start()
    barrier = pltpu.get_barrier_semaphore()

    def greet(i, carry):
        pl.semaphore_signal(barrier, inc=1, device_id=other(i), device_id_type=MESH)
        return carry

    lax.fori_loop(1, ns * nb, greet, 0)
    pl.semaphore_wait(barrier, ns * nb - 1)

    pending = []

    def remote(src, dst, ssem, rsem, dev):
        c = pltpu.make_async_remote_copy(
            src_ref=src, dst_ref=dst, send_sem=ssem, recv_sem=rsem,
            device_id=dev, device_id_type=MESH)
        c.start()
        pending.append(c)
        return c

    near = jnp.minimum(z, nz - 1 - z)

    def zk(t):
        if t == 0:
            return z
        both = t <= 2 * near
        dist = jnp.where(both, (t + 1) // 2, t - near)
        above = jnp.where(both, t % 2, jnp.where(z < nz - 1 - z, 1, 0))
        return z + dist * (2 * above - 1)

    def z_copy(t, up):
        src = zk(t)
        to = jnp.minimum(z + 1, nz - 1) if up else jnp.maximum(z - 1, 0)
        return pltpu.make_async_remote_copy(
            src_ref=shard(t), dst_ref=wg.at[wrows(seq, src)],
            send_sem=z_s.at[nz * up + src], recv_sem=z_r.at[src],
            device_id=(seq, to * 2 + core), device_id_type=MESH)

    def z_pass(t, up):
        src = zk(t)
        if up:
            return jnp.logical_and(src <= z, z < nz - 1)
        return jnp.logical_and(src >= z, z > 0)

    def z_each(t, act):
        for up in (0, 1):
            @pl.when(z_pass(t, up))
            def _():
                act(z_copy(t, up))

    def wrows(s, zz):
        return pl.ds(pl.multiple_of((s * nb + zz * 2 + core) * r, 16), r)

    def shard(k):
        return w_ref if k == 0 else wg.at[wrows(seq, zk(k))]

    own = wrows(seq, z)
    hc, lc, dac, dbc, cc = {}, {}, {}, {}, {}

    def plane_send(k):
        rows = wrows(seq, zk(k))
        hc[k] = remote(shard(k), wg.at[rows], p_s.at[2 * k], p_r.at[2 * k], hi_dev)
        lc[k] = remote(shard(k), wg.at[rows], p_s.at[2 * k + 1], p_r.at[2 * k + 1], lo_dev)

    def core_send(k, j, s):
        rows = wrows(s, zk(k))
        src = w_ref if (k == 0 and j == 0) else wg.at[rows]
        i = 4 * k + j
        cc[i] = remote(src, wg.at[rows], c_s.at[i], c_r.at[i], core_dev)

    def z_arrive(k):
        z_copy(k, 0).wait_recv()
        z_each(k, lambda c: c.start())
        plane_send(k)
        core_send(k, 0, seq)

    def plane_arrive(k):
        hc[k].wait_recv()
        v = wg.at[wrows(sh, zk(k)), cols_a]
        dac[k] = remote(v, v, d_s.at[2 * k], d_r.at[2 * k], lo_dev)
        lc[k].wait_recv()
        v = wg.at[wrows(sl, zk(k)), cols_b]
        dbc[k] = remote(v, v, d_s.at[2 * k + 1], d_r.at[2 * k + 1], hi_dev)
        core_send(k, 1, sh)
        core_send(k, 2, sl)

    def diag_arrive(k):
        dac[k].wait_recv()
        dbc[k].wait_recv()
        core_send(k, 3, sd)

    xa = remote(attn_hbm, rx_attn, x_s.at[0], x_r.at[0], core_dev)
    plane_send(0)
    z_each(0, lambda c: c.start())
    xo = remote(og_hbm, rx_og, x_s.at[1], x_r.at[1], core_dev)
    core_send(0, 0, seq)
    wg[own, :] = w_ref[...]

    def transpose_in(src, koff):
        for s in range(ns):
            tbuf[...] = src[:, s * block:(s + 1) * block].T
            for zz in range(nz):
                part = tbuf[pl.ds(pl.multiple_of((zz * 2 + core) * r, 16), r), :]
                attn_t[pl.ds((s * nz + zz) * r, r), pl.ds(koff, tok)] = part

    tile = 256 if dout % 256 == 0 and din % 256 == 0 else 128
    ntile = dout // tile

    def grad_tiles(first, last):
        def body(i, carry):
            c = pl.ds(pl.multiple_of(i * tile, tile), tile)
            acc = jnp.dot(attn_t[:, :tok], og_ref[:, c], preferred_element_type=F32)
            acc += jnp.dot(attn_t[:, tok:], rx_og[:, c], preferred_element_type=F32)
            g[:, c] = acc.astype(BF16)
            return carry
        lax.fori_loop(first, last, body, 0)

    la.wait()
    transpose_in(attn_ref, 0)
    if nz > 1:
        z_arrive(1)
    xa.wait_recv()
    transpose_in(rx_attn, tok)
    plane_arrive(0)
    xo.wait_recv()
    lg.wait()
    for k in range(1, nz):
        grad_tiles((k - 1) * ntile // (nz - 1), k * ntile // (nz - 1))
        if k + 1 < nz:
            z_arrive(k + 1)
        if k < nz - 1:
            plane_arrive(k)

    def grows(s, i):
        return pl.ds(pl.multiple_of((s * nz + lax.rem(z + 1 + i, nz)) * r, 16), r)

    def rr(i):
        return pl.ds(i * r, r)

    s1, s2 = {}, {}

    def stage1(i):
        s1[i] = [
            remote(g.at[grows(sd, i), cols_a], r1a.at[rr(2 * i + 1)], s1_s.at[4 * i], s1_r.at[4 * i], hi_dev),
            remote(g.at[grows(sd, i), cols_b], r1b.at[rr(2 * i + 1)], s1_s.at[4 * i + 1], s1_r.at[4 * i + 1], lo_dev),
            remote(g.at[grows(sh, i), cols_a], r1a.at[rr(2 * i)], s1_s.at[4 * i + 2], s1_r.at[4 * i + 2], hi_dev),
            remote(g.at[grows(sl, i), cols_b], r1b.at[rr(2 * i)], s1_s.at[4 * i + 3], s1_r.at[4 * i + 3], lo_dev),
        ]

    def stage2(i):
        s1[i][0].wait_recv()
        t2[rr(i), cols_a] = (g[grows(sl, i), cols_a].astype(F32) + r1a[rr(2 * i + 1), :].astype(F32)).astype(BF16)
        ca = remote(t2.at[rr(i), cols_a], r2.at[rr(i), cols_a], s2_s.at[2 * i], s2_r.at[2 * i], lo_dev)
        s1[i][1].wait_recv()
        t2[rr(i), cols_b] = (g[grows(sh, i), cols_b].astype(F32) + r1b[rr(2 * i + 1), :].astype(F32)).astype(BF16)
        cb = remote(t2.at[rr(i), cols_b], r2.at[rr(i), cols_b], s2_s.at[2 * i + 1], s2_r.at[2 * i + 1], hi_dev)
        s2[i] = [ca, cb]

    zsum = {}

    def stage3(i):
        for c in (s1[i][2], s1[i][3], s2[i][0], s2[i][1]):
            c.wait_recv()
        for cols, r1 in ((cols_a, r1a), (cols_b, r1b)):
            v = g[grows(seq, i), cols].astype(F32) + r1[rr(2 * i), :].astype(F32) + r2[rr(i), cols].astype(F32)
            if i == nz - 1:
                gw_ref[:, cols] = v
            else:
                pz[rr(i), cols] = v.astype(BF16)
        if i < nz - 1:
            dev = (seq, lax.rem(z + 1 + i, nz) * 2 + core)
            zsum[i] = remote(pz.at[rr(i)], rz.at[rr(i)], rz_s.at[i], rz_r.at[i], dev)

    stage1(0)
    if nz > 1:
        plane_arrive(nz - 1)
    for k in range(nz):
        diag_arrive(k)
        if k == 0 and nz > 1:
            stage1(1)

    def input_tiles(first, last):
        def body(i, carry):
            c = pl.ds(pl.multiple_of(i * tile, tile), tile)
            v = lax.dot_general(og_ref[...], wg[c, :], (((1,), (1,)), ((), ())), preferred_element_type=F32)
            ig_ref[:, c] = v.astype(BF16)
            return carry
        lax.fori_loop(first, last, body, 0)

    itile = din // tile
    stage2(0)
    for i in range(4 * nz):
        cc[i].wait_recv()
    for i in range(nz):
        input_tiles(i * itile // nz, (i + 1) * itile // nz)
        if i + 2 < nz:
            stage1(i + 2)
        if i + 1 < nz:
            stage2(i + 1)
        stage3(i)
    for i in range(nz - 1):
        zsum[i].wait_recv()
        gw_ref[...] += rz[rr(i), :].astype(F32)

    v = gw_ref[...]
    part = jnp.sum((v * v).reshape(r // 8, 8, dout), axis=0)
    acc = part[:, :128]
    for i in range(1, dout // 128):
        acc += part[:, i * 128:(i + 1) * 128]
    sqs[0] = acc

    def q_copy(i):
        return pltpu.make_async_remote_copy(
            src_ref=sqs.at[0], dst_ref=sqs.at[i], send_sem=q_s.at[i], recv_sem=q_r.at[i],
            device_id=other(i), device_id_type=MESH)

    def q_start(i, carry):
        q_copy(i).start()
        return carry

    def q_wait(i, carry):
        q_copy(i).wait()
        return carry

    lax.fori_loop(1, ns * nb, q_start, 0)
    lax.fori_loop(1, ns * nb, q_wait, 0)
    total = sqs[0]
    for i in range(1, ns * nb):
        total += sqs[i]
    sq_ref[...] = total
    for c in pending:
        c.wait_send()
    for t in range(nz):
        z_each(t, lambda c: c.wait_send())


def fused(attn_out, out_grad, shard_weight, ns, nb):
    tok, din = attn_out.shape
    dout = out_grad.shape[1]
    r = shard_weight.shape[0]
    nz = nb // 2
    n = ns * nb
    dma = lambda k: pltpu.SemaphoreType.DMA((k,))
    vm = pl.BlockSpec(memory_space=pltpu.VMEM)
    pairs = [2, 2 * nz, 2 * nz, 2 * nz, 4 * nz, 4 * nz, 2 * nz, nz, n]
    return pl.pallas_call(
        functools.partial(kernel, nb),
        out_shape=(
            jax.ShapeDtypeStruct((tok, din), BF16),
            jax.ShapeDtypeStruct((r, dout), F32),
            jax.ShapeDtypeStruct((8, 128), F32),
        ),
        in_specs=[pl.BlockSpec(memory_space=pl.ANY)] * 2 + [vm],
        out_specs=(vm,) * 3,
        scratch_shapes=[
            pltpu.VMEM((tok, din), BF16),
            pltpu.VMEM((tok, dout), BF16),
            dma(2),
            pltpu.VMEM((tok, din), BF16),
            pltpu.VMEM((tok, dout), BF16),
            pltpu.VMEM((nb * r, tok), BF16),
            pltpu.VMEM((din // 2, 2 * tok), BF16),
            pltpu.VMEM((din, dout), BF16),
            pltpu.VMEM((din // 2, dout), BF16),
            pltpu.VMEM((2 * nz * r, dout // 2), BF16),
            pltpu.VMEM((2 * nz * r, dout // 2), BF16),
            pltpu.VMEM((nz * r, dout), BF16),
            pltpu.VMEM((nz * r, dout), BF16),
            pltpu.VMEM((nz * r, dout), BF16),
            pltpu.VMEM((nz * r, dout), BF16),
            pltpu.VMEM((n, 8, 128), F32),
        ] + [dma(k) for k in pairs for _ in range(2)],
        compiler_params=pltpu.CompilerParams(
            collective_id=0, has_side_effects=True, vmem_limit_bytes=66_000_000),
    )(attn_out, out_grad, shard_weight)


def plain(attn_out, out_grad, shard_weight):
    projected = lax.dot_general(
        out_grad,
        lax.all_gather(shard_weight, ("seq", "batch"), axis=0, tiled=True),
        (((1,), (1,)), ((), ())),
        preferred_element_type=F32,
    )
    width = out_grad.shape[1] // GRAD_BLOCKS
    parts = []
    for b in range(GRAD_BLOCKS):
        d = lax.dot_general(
            attn_out, out_grad[:, b * width:(b + 1) * width],
            (((0,), (0,)), ((), ())), preferred_element_type=F32).astype(BF16)
        d = lax.psum_scatter(d, "seq", scatter_dimension=0, tiled=True)
        parts.append(lax.psum_scatter(d, "batch", scatter_dimension=0, tiled=True).astype(F32))
    weight_grad = jnp.concatenate(parts, axis=1)
    squares = lax.psum(jnp.sum(weight_grad * weight_grad), ("seq", "batch"))
    return projected.astype(BF16), weight_grad, squares


def on_device(ns, nb, attn_out, out_grad, master, moment_one, moment_two):
    shard_weight = master.astype(BF16)
    r, dout = master.shape
    din = attn_out.shape[1]
    if ns == 4 and nb % 2 == 0 and r % 16 == 0 and (nb * r) % 128 == 0 and dout % 256 == 0:
        input_grad, weight_grad, sq = fused(attn_out, out_grad, shard_weight, ns, nb)
        squares = jnp.sum(sq)
    else:
        input_grad, weight_grad, squares = plain(attn_out, out_grad, shard_weight)
    grad_norm = jnp.sqrt(squares) + 1e-06
    limit = jnp.sqrt(jnp.float32(din * dout))
    clipped = weight_grad * jnp.minimum(jnp.float32(1.0), limit / grad_norm)
    new_one = 0.9 * moment_one + 0.1 * clipped
    new_two = 0.999 * moment_two + 0.001 * clipped * clipped
    first_hat = new_one / (1.0 - 0.9**STEP)
    second_hat = new_two / (1.0 - 0.999**STEP)
    new_master = master - 0.01 * (first_hat / (jnp.sqrt(second_hat) + 1e-08) + 0.1 * master)
    return (input_grad, new_master, new_one, new_two)


def solution(mesh):
    spec = P(("seq", "batch"), None)
    return jax.shard_map(
        functools.partial(on_device, mesh.shape["seq"], mesh.shape["batch"]),
        mesh=mesh,
        in_specs=(spec,) * 5,
        out_specs=(spec,) * 4,
        check_vma=False,
    )
```

profile of v0, /device:TPU:0, one launch (start us, length us, event | category | flops | bytes accessed | tf_op | source)
XLA Modules:
  0.0 144.5 jit_solution(1295256225076843471)
XLA Ops:
  0.6 1.9 %convert_element_type.3.w_ref = bf16[80,2560]{1,0:T(8,128)(2,1)} convert(f32[80,2560]{1,0:T(8,128)} %param.7) | non-fusion elementwise | flops 204800 | bytes 1228800 | tf_op jit(solution)/shard_map/convert_element_type | solution.py:347
  2.6 0.0 copy-start
  2.6 134.7 %shard_map.84 = (bf16[512,2560]{1,0:T(8,128)(2,1)}, f32[80,2560]{1,0:T(8,128)}, f32[8,128]{1,0:T(8,128)}) custom-call(bf16[512,2560]{1,0:T(8,128)(2,1)} %attn_hbm.1, bf16[512,2560]{1,0:T(8,128)(2,1)} %og_hbm.1, bf16[80,2560]{1,0:T(8,128)(2,1)} %convert_element_type.3.w_ref), custom_call_target="tpu_custom_call" | custom-call | tf_op jit(solution)/shard_map/pallas_call | solution.py:294
  137.3 1.3 reduce_sum.9
  139.3 0.0 copy-done
  139.3 0.0 copy-start.1
  139.4 3.7 %multiply_subtract_fusion = (f32[80,2560]{1,0:T(8,128)}, f32[80,2560]{1,0:T(8,128)}, f32[80,2560]{1,0:T(8,128)}) fusion(f32[80,2560]{1,0:T(8,128)S(1)} %copy-done, f32[80,2560]{1,0:T(8,128)} %get-tuple-element.8, f32[]{:T(128)S(6)} %min_shard_map.3, f32[80,2560]{1,0:T(8,128)} %param.8, f32[80,2560]{1,0:T(8,128)} %param.9), kind=kLoop, calls=%fused_computation.2 | loop fusion | flops 3276800 | bytes 5734404 | tf_op jit(solution)/shard_map/sub | solution.py:362
  143.0 0.0 copy-done.1
  143.0 1.5 %copy.10 = bf16[512,2560]{1,0:T(8,128)(2,1)} copy(bf16[512,2560]{1,0:T(8,128)(2,1)S(1)} %copy-done.1) | data formatting | bytes 5242880
Async XLA Ops:
  2.6 136.8 %copy-start = (f32[80,2560]{1,0:T(8,128)S(1)}, f32[80,2560]{1,0:T(8,128)}, u32[]{:S(2)}) copy-start(f32[80,2560]{1,0:T(8,128)} %param.7) | copy-start | bytes 2457604
  139.3 3.7 %copy-start.1 = (bf16[512,2560]{1,0:T(8,128)(2,1)S(1)}, bf16[512,2560]{1,0:T(8,128)(2,1)}, u32[]{:S(2)}) copy-start(bf16[512,2560]{1,0:T(8,128)(2,1)} %get-tuple-element.17) | copy-start | bytes 7864324
where the time goes:
time: 145 us
  Pallas kernels  135 us (93%)
  other arithmetic  6.88 us (5%)
  local copies, waits for them, and re-layouts  1.5 us (1%)
    pallas_call x1, Pallas kernels, fused(): pl.pallas_call(functools.partial(kernel, nb), out_shape=(jax.ShapeDtypeSt...  135 us
    sub x1, other arithmetic, on_device(): master - 0.01 * (first_hat / (jnp.sqrt(second_hat) + 1e-08) + 0.1 * master)  3.65 us

commit v1 on v0

v1 whole, which is shorter than its diff:
```python
import functools
import jax
import jax.numpy as jnp
from jax import lax
from jax.experimental import pallas as pl
from jax.experimental.pallas import tpu as pltpu
from jax.sharding import PartitionSpec as P

GRAD_BLOCKS = 4
STEP = 10
MESH = pl.DeviceIdType.MESH
F32 = jnp.float32
BF16 = jnp.bfloat16


def kernel(nb, attn_hbm, og_hbm, master_hbm, ig_hbm, gw_ref, sq_ref,
           attn_ref, og_ref, mst, rx_og, tbuf, tx, at_own, at_rx, wg, g, rx1, rzb, rx3, fbuf, ig, sqs,
           l_s, o_s, x_s, x_r, p_s, p_r, z_s, z_r, e_s, e_r, c_s, c_r, r_s, r_r, y_s, y_r, f_s, f_r, q_s, q_r):
    ns = 4
    nz = nb // 2
    tok, din = attn_ref.shape
    dout = og_ref.shape[1]
    r = gw_ref.shape[0]
    half = dout // 2
    block = nb * r
    seq = lax.axis_index("seq")
    batch = lax.axis_index("batch")
    z = batch // 2
    core = batch % 2
    hi = seq // 2
    lo = seq % 2
    sh = (1 - hi) * 2 + lo
    sl = hi * 2 + (1 - lo)
    sd = (1 - hi) * 2 + (1 - lo)
    first = (sl, sh)
    last = (sh, sl)
    cols = (pl.ds(0, half), pl.ds(half, half))
    core_dev = (seq, z * 2 + 1 - core)
    edge = jnp.logical_or(z == 0, z == nz - 1)

    def other(i):
        f = lax.rem(seq * nb + batch + i, ns * nb)
        return (f // nb, lax.rem(f, nb))

    lm = pltpu.make_async_copy(master_hbm, mst, l_s.at[2])
    lm.start()
    la = pltpu.make_async_copy(attn_hbm, attn_ref, l_s.at[0])
    la.start()
    lg = pltpu.make_async_copy(og_hbm, og_ref, l_s.at[1])
    lg.start()
    barrier = pltpu.get_barrier_semaphore()

    def greet(i, carry):
        pl.semaphore_signal(barrier, inc=1, device_id=other(i), device_id_type=MESH)
        return carry

    lax.fori_loop(1, ns * nb, greet, 0)

    near = jnp.minimum(z, nz - 1 - z)

    def zk(t):
        if t == 0:
            return z
        both = t <= 2 * near
        dist = jnp.where(both, (t + 1) // 2, t - near)
        above = jnp.where(both, t % 2, jnp.where(z < nz - 1 - z, 1, 0))
        return z + dist * (2 * above - 1)

    def wrows(s, zz):
        return pl.ds(pl.multiple_of((s * nb + zz * 2 + core) * r, 16), r)

    def grows(s, zz):
        return pl.ds(pl.multiple_of((zz * ns + s) * r, 16), r)

    def remote(s, d, ssem, rsem, dev):
        return pltpu.make_async_remote_copy(
            src_ref=s, dst_ref=d, send_sem=ssem, recv_sem=rsem,
            device_id=dev, device_id_type=MESH)

    def shard(s, zz, h):
        return wg.at[wrows(s, zz), cols[h]]

    def p_copy(h):
        v = shard(seq, z, h)
        return remote(v, v, p_s.at[h], p_r.at[h], (first[h], batch))

    def z_copy(h, i, t, up):
        zz = zk(t)
        to = jnp.minimum(z + 1, nz - 1) if up else jnp.maximum(z - 1, 0)
        v = shard((seq, first[h])[i], zz, h)
        k = (h * 2 + i) * nz + zz
        return remote(v, v, z_s.at[4 * nz * up + k], z_r.at[k], (seq, to * 2 + core))

    def z_each(h, i, t, act):
        zz = zk(t)
        for up in (0, 1):
            ok = jnp.logical_and(zz <= z, z < nz - 1) if up else jnp.logical_and(zz >= z, z > 0)

            @pl.when(ok)
            def _():
                act(z_copy(h, i, t, up))

    def e_copy(h, i, t):
        v = shard((seq, first[h])[i], zk(t), h)
        k = (h * 2 + i) * nz + t
        return remote(v, v, e_s.at[k], e_r.at[k], (last[h], batch))

    def c_copy(k, t):
        s, h = ((seq, None), (sl, 0), (sh, 1), (sh, 0), (sd, 0), (sl, 1), (sd, 1))[k]
        v = wg.at[wrows(s, zk(t))] if h is None else shard(s, zk(t), h)
        return remote(v, v, c_s.at[7 * t + k], c_r.at[7 * t + k], core_dev)

    def r_copy(h, i, j):
        k = (h * 2 + i) * nz + j
        v = g.at[grows((last[h], sd)[i], zk(nz - 1 - j)), cols[h]]
        return remote(v, rx1.at[k], r_s.at[k], r_r.at[k], (last[h], batch))

    def y_copy(h, i, j):
        t = zk(nz - 1 - j)
        up = t > z
        to = jnp.where(up, jnp.minimum(z + 1, nz - 1), jnp.maximum(z - 1, 0))
        k = (h * 2 + i) * (nz + 1) + jnp.where(jnp.logical_and(jnp.logical_not(up), t == z - 1), nz, t)
        v = g.at[grows((seq, first[h])[i], t), cols[h]]
        return remote(v, rzb.at[k], y_s.at[(h * 2 + i) * nz + j], y_r.at[k], (seq, to * 2 + core))

    def y_slot(h, i, t):
        k = (h * 2 + i) * (nz + 1) + t
        v = g.at[grows(seq, z), cols[h]]
        return remote(v, rzb.at[k], y_s.at[0], y_r.at[k], core_dev), rzb.at[k]

    def f_copy(h):
        v = g.at[grows(first[h], z), cols[h]]
        return remote(v, rx3.at[h], f_s.at[h], f_r.at[h], (first[h], batch))

    def az(t, h, i):
        z_copy(h, i, t, 0).wait_recv()
        z_each(h, i, t, lambda c: c.start())
        e_copy(h, i, t).start()
        if i == 1:
            c_copy(1 + h, t).start()
        elif h == 1:
            c_copy(0, t).start()

    def ae(t, h, i):
        e_copy(h, i, t).wait_recv()
        c_copy(3 + 2 * h + i, t).start()

    def rs(j):
        for i in (1, 0):
            for h in (0, 1):
                r_copy(h, i, j).start()

    def rr(j, h, i):
        k = (h * 2 + i) * nz + j
        t = zk(nz - 1 - j)
        rows = grows((seq, first[h])[i], t)
        r_copy(h, i, j).wait_recv()
        more = jnp.logical_or(jnp.logical_and(t > z, z > 0), jnp.logical_and(t < z, z < nz - 1))

        @pl.when(more)
        def _():
            c, buf = y_slot(h, i, t)
            c.wait_recv()
            g[rows, cols[h]] = (g[rows, cols[h]].astype(F32) + rx1[k].astype(F32) + buf[...].astype(F32)).astype(BF16)

        @pl.when(jnp.logical_not(more))
        def _():
            g[rows, cols[h]] = (g[rows, cols[h]].astype(F32) + rx1[k].astype(F32)).astype(BF16)
        y_copy(h, i, j).start()

    def rl(h, i):
        j = nz - 1
        k = (h * 2 + i) * nz + j
        rows = grows((seq, first[h])[i], z)
        dst = gw_ref.at[:, cols[h]] if i == 0 else fbuf.at[h]
        r_copy(h, i, j).wait_recv()
        dst[...] = g[rows, cols[h]].astype(F32) + rx1[k].astype(F32)
        for ok, t in ((z > 0, z), (z < nz - 1, nz)):
            @pl.when(ok)
            def _():
                c, buf = y_slot(h, i, t)
                c.wait_recv()
                dst[...] += buf[...].astype(F32)
        if i == 1:
            g[rows, cols[h]] = dst[...].astype(BF16)
            f_copy(h).start()

    tile = 256

    def grad(j):
        rows = pl.ds(pl.multiple_of(zk(nz - 1 - j) * (ns * r), 16), ns * r)

        def body(i, carry):
            c = pl.ds(pl.multiple_of(i * tile, tile), tile)
            acc = jnp.dot(at_own[rows, :], og_ref[:, c], preferred_element_type=F32)
            acc += jnp.dot(at_rx[rows, :], rx_og[:, c], preferred_element_type=F32)
            g[rows, c] = acc.astype(BF16)
            return carry
        lax.fori_loop(0, dout // tile, body, 0)

    def input_cols(q, s):
        def part(c):
            v = lax.dot_general(og_ref[...], wg[c, :], (((1,), (1,)), ((), ())), preferred_element_type=F32)
            ig[:, c] = v.astype(BF16)

        def body(i, carry):
            part(pl.ds(pl.multiple_of(s * block + i * tile, 128), tile))
            return carry
        lax.fori_loop(0, block // tile, body, 0)
        if block % tile:
            part(pl.ds(pl.multiple_of(s * block + block // tile * tile, 128), block % tile))
        o_copy(q, s).start()

    def o_copy(q, s):
        c = pl.ds(pl.multiple_of(s * block, 128), block)
        return pltpu.make_async_copy(ig.at[:, c], ig_hbm.at[:, c], o_s.at[q])

    xo = remote(og_hbm, rx_og, x_s.at[0], x_r.at[0], core_dev)
    xt = remote(tx, at_rx, x_s.at[1], x_r.at[1], core_dev)

    lm.wait()
    wg[wrows(seq, z), :] = mst[...].astype(BF16)
    pl.semaphore_wait(barrier, ns * nb - 1)
    for h in (0, 1):
        p_copy(h).start()
    for h in (0, 1):
        z_each(h, 0, 0, lambda c: c.start())
    for h in (1, 0):
        e_copy(h, 0, 0).start()
    xo.start()
    la.wait()
    for s in range(ns):
        tbuf[...] = attn_ref[:, s * block:(s + 1) * block].T
        for zz in range(nz):
            rows = pl.ds((zz * ns + s) * r, r)
            at_own[rows, :] = tbuf[pl.ds(pl.multiple_of((zz * 2 + core) * r, 16), r), :]
            tx[rows, :] = tbuf[pl.ds(pl.multiple_of((zz * 2 + 1 - core) * r, 16), r), :]
    xt.start()
    c_copy(0, 0).start()
    for h in (0, 1):
        p_copy(h).wait_recv()
        z_each(h, 1, 0, lambda c: c.start())
        e_copy(h, 1, 0).start()
        c_copy(1 + h, 0).start()
    lg.wait()
    xo.wait_recv()
    xt.wait_recv()

    def do(on_edge, inside):
        for ok, events in ((edge, on_edge), (jnp.logical_not(edge), inside)):
            if events:
                @pl.when(ok)
                def _():
                    for f, *a in events:
                        f(*a)

    hs = (0, 1)
    ih = [(h, i) for i in (1, 0) for h in hs]
    grad(0)
    rs(0)
    do([(az, 1, h, 0) for h in hs],
       [(az, t, h, 0) for h in hs for t in (1, 2)])
    grad(1)
    do([(az, 1, 0, 1)],
       [(az, t, 0, 1) for t in (1, 2)])
    grad(2)
    do([(az, 1, 1, 1), (rs, 1)],
       [(az, t, 1, 1) for t in (1, 2)] + [(rs, 1), (rs, 2)])
    do([(rr, 0, h, i) for h, i in ih[:2]], [])
    grad(3)
    do([(rr, 0, h, i) for h, i in ih[2:]]
       + [(az, 2, h, i) for i in hs for h in hs]
       + [(rs, 2)]
       + [(rr, 1, h, i) for h, i in ih]
       + [(ae, t, h, i) for t in (0, 1) for i in hs for h in hs]
       + [(az, 3, h, i) for i in hs for h in hs]
       + [(rs, 3)]
       + [(ae, 2, h, i) for i in hs for h in hs],
       [e for n, (h, i) in enumerate(ih) for e in ((az, 3, n % 2, n // 2), (rr, 0, h, i))]
       + [(rs, 3)]
       + [(ae, t, h, i) for t in (0, 1, 2) for i in hs for h in hs]
       + [(rr, j, h, i) for h, i in ih[:2] for j in (1, 2)])
    for t in range(nz):
        c_copy(0, t).wait_recv()
    do([], [(rr, j, h, i) for h, i in ih[2:] for j in (1, 2)])
    input_cols(0, seq)
    do([(rr, 2, h, i) for h, i in ih], [])
    for i in hs:
        for h in hs:
            ae(3, h, i)
    for k in range(1, 7):
        for t in range(nz):
            c_copy(k, t).wait_recv()
    input_cols(1, sl)
    input_cols(2, sh)
    rl(0, 1)
    rl(1, 1)
    input_cols(3, sd)
    rl(0, 0)
    rl(1, 0)
    for h in hs:
        f_copy(h).wait_recv()
        gw_ref[:, cols[h]] += rx3[h].astype(F32)

    v = gw_ref[...]
    part = jnp.sum((v * v).reshape(r // 8, 8, dout), axis=0)
    acc = part[:, :128]
    for i in range(1, dout // 128):
        acc += part[:, i * 128:(i + 1) * 128]
    sqs[0] = jnp.sum(acc, axis=0, keepdims=True)

    def q_copy(i):
        return remote(sqs.at[0], sqs.at[i], q_s.at[i], q_r.at[i], other(i))

    def q_start(i, carry):
        q_copy(i).start()
        return carry

    def q_wait(i, carry):
        q_copy(i).wait()
        return carry

    lax.fori_loop(1, ns * nb, q_start, 0)
    for h in hs:
        p_copy(h).wait_send()
        f_copy(h).wait_send()
        for i in hs:
            for t in range(nz):
                z_each(h, i, t, lambda c: c.wait_send())
                e_copy(h, i, t).wait_send()
                r_copy(h, i, t).wait_send()
                if t < nz - 1:
                    y_copy(h, i, t).wait_send()
    for t in range(nz):
        for k in range(7):
            c_copy(k, t).wait_send()
    xo.wait_send()
    xt.wait_send()
    for q, s in enumerate((seq, sl, sh, sd)):
        o_copy(q, s).wait()
    lax.fori_loop(1, ns * nb, q_wait, 0)
    total = sqs[0]
    for i in range(1, ns * nb):
        total += sqs[i]
    sq_ref[...] = total


def fused(attn_out, out_grad, master, ns, nb):
    tok, din = attn_out.shape
    dout = out_grad.shape[1]
    r = master.shape[0]
    half = dout // 2
    nz = nb // 2
    n = ns * nb
    dma = lambda k: pltpu.SemaphoreType.DMA((k,))
    vm = pl.BlockSpec(memory_space=pltpu.VMEM)
    hbm = pl.BlockSpec(memory_space=pl.ANY)
    sems = [3, 4, 2, 2, 2, 2, 8 * nz, 4 * nz, 4 * nz, 4 * nz, 7 * nz, 7 * nz,
            4 * nz, 4 * nz, 4 * nz, 4 * (nz + 1), 2, 2, n, n]
    return pl.pallas_call(
        functools.partial(kernel, nb),
        out_shape=(
            jax.ShapeDtypeStruct((tok, din), BF16),
            jax.ShapeDtypeStruct((r, dout), F32),
            jax.ShapeDtypeStruct((1, 128), F32),
        ),
        in_specs=[hbm] * 3,
        out_specs=(hbm, vm, vm),
        scratch_shapes=[
            pltpu.VMEM((tok, din), BF16),
            pltpu.VMEM((tok, dout), BF16),
            pltpu.VMEM((r, dout), F32),
            pltpu.VMEM((tok, dout), BF16),
            pltpu.VMEM((nb * r, tok), BF16),
            pltpu.VMEM((din // 2, tok), BF16),
            pltpu.VMEM((din // 2, tok), BF16),
            pltpu.VMEM((din // 2, tok), BF16),
            pltpu.VMEM((din, dout), BF16),
            pltpu.VMEM((din // 2, dout), BF16),
            pltpu.VMEM((4 * nz, r, half), BF16),
            pltpu.VMEM((4 * (nz + 1), r, half), BF16),
            pltpu.VMEM((2, r, half), BF16),
            pltpu.VMEM((2, r, half), F32),
            pltpu.VMEM((tok, din), BF16),
            pltpu.VMEM((n, 1, 128), F32),
        ] + [dma(k) for k in sems],
        compiler_params=pltpu.CompilerParams(
            collective_id=0, has_side_effects=True, vmem_limit_bytes=62_000_000),
    )(attn_out, out_grad, master)


def plain(attn_out, out_grad, shard_weight):
    projected = lax.dot_general(
        out_grad,
        lax.all_gather(shard_weight, ("seq", "batch"), axis=0, tiled=True),
        (((1,), (1,)), ((), ())),
        preferred_element_type=F32,
    )
    width = out_grad.shape[1] // GRAD_BLOCKS
    parts = []
    for b in range(GRAD_BLOCKS):
        d = lax.dot_general(
            attn_out, out_grad[:, b * width:(b + 1) * width],
            (((0,), (0,)), ((), ())), preferred_element_type=F32).astype(BF16)
        d = lax.psum_scatter(d, "seq", scatter_dimension=0, tiled=True)
        parts.append(lax.psum_scatter(d, "batch", scatter_dimension=0, tiled=True).astype(F32))
    weight_grad = jnp.concatenate(parts, axis=1)
    squares = lax.psum(jnp.sum(weight_grad * weight_grad), ("seq", "batch"))
    return projected.astype(BF16), weight_grad, squares


def on_device(ns, nb, attn_out, out_grad, master, moment_one, moment_two):
    r, dout = master.shape
    din = attn_out.shape[1]
    if ns == 4 and nb == 8 and r % 16 == 0 and (nb * r) % 128 == 0 and dout % 256 == 0:
        input_grad, weight_grad, sq = fused(attn_out, out_grad, master, ns, nb)
        squares = jnp.sum(sq)
    else:
        input_grad, weight_grad, squares = plain(attn_out, out_grad, master.astype(BF16))
    grad_norm = jnp.sqrt(squares) + 1e-06
    limit = jnp.sqrt(jnp.float32(din * dout))
    clipped = weight_grad * jnp.minimum(jnp.float32(1.0), limit / grad_norm)
    new_one = 0.9 * moment_one + 0.1 * clipped
    new_two = 0.999 * moment_two + 0.001 * clipped * clipped
    first_hat = new_one / (1.0 - 0.9**STEP)
    second_hat = new_two / (1.0 - 0.999**STEP)
    new_master = master - 0.01 * (first_hat / (jnp.sqrt(second_hat) + 1e-08) + 0.1 * master)
    return (input_grad, new_master, new_one, new_two)


def solution(mesh):
    spec = P(("seq", "batch"), None)
    return jax.shard_map(
        functools.partial(on_device, mesh.shape["seq"], mesh.shape["batch"]),
        mesh=mesh,
        in_specs=(spec,) * 5,
        out_specs=(spec,) * 4,
        check_vma=False,
    )
```

time: 145 us -> 102 us (0.70)
  Pallas kernels: 135 us -> 94.3 us
  other arithmetic: 6.88 us -> 4.42 us
    pallas_call x1, Pallas kernels: 135 us -> 94.3 us  [fused(): pl.pallas_call(functools.partial(kernel, nb), out_shape=(jax.ShapeDtypeSt...]
    convert_element_type x1 -> x0, other arithmetic: 1.94 us -> none  [on_device(): shard_weight = master.astype(BF16)]
where the time goes in v1:
time: 102 us
  Pallas kernels  94.3 us (92%)
  other arithmetic  4.42 us (4%)
  local copies, waits for them, and re-layouts  1.51 us (1%)
  between operations  1.43 us (1%)
    pallas_call x1, Pallas kernels, fused(): pl.pallas_call(functools.partial(kernel, nb), out_shape=(jax.ShapeDtypeSt...  94.3 us
    sub x1, other arithmetic, on_device(): master - 0.01 * (first_hat / (jnp.sqrt(second_hat) + 1e-08) + 0.1 * master)  3.14 us

profile of v1, /device:TPU:0, one launch (start us, length us, event | category | flops | bytes accessed | tf_op | source)
XLA Modules:
  0.0 101.7 jit_solution(2192033656934646791)
XLA Ops:
  0.6 0.0 copy-start
  0.6 0.0 copy-start.3
  0.7 0.0 copy-start.2
  0.7 94.3 %shard_map.84 = (bf16[512,2560]{1,0:T(8,128)(2,1)}, f32[80,2560]{1,0:T(8,128)}, f32[1,128]{1,0:T(1,128)}) custom-call(bf16[512,2560]{1,0:T(8,128)(2,1)} %attn_hbm.1, bf16[512,2560]{1,0:T(8,128)(2,1)} %og_hbm.1, f32[80,2560]{1,0:T(8,128)} %master_hbm.1), custom_call_target="tpu_custom_call" | custom-call | tf_op jit(solution)/shard_map/pallas_call | solution.py:360
  95.0 1.3 %reduce_sum.9 = f32[]{:T(128)} reduce(f32[1,128]{1,0:T(1,128)} %get-tuple-element.9, f32[]{:T(128)} %constant.4.clone.1), dimensions={0,1}, to_apply=%region_0.0 | reduce | flops 127 | bytes 520 | tf_op jit(solution)/shard_map/reduce_sum | solution.py:417
  97.0 0.0 copy-done
  97.0 0.0 copy-done.3
  97.0 0.0 copy-done.2
  97.0 0.0 copy-start.1
  97.1 3.1 %multiply_subtract_fusion = (f32[80,2560]{1,0:T(8,128)}, f32[80,2560]{1,0:T(8,128)}, f32[80,2560]{1,0:T(8,128)}) fusion(f32[80,2560]{1,0:T(8,128)S(1)} %copy-done, f32[80,2560]{1,0:T(8,128)} %get-tuple-element.8, f32[]{:T(128)S(6)} %min_shard_map.3, f32[80,2560]{1,0:T(8,128)S(1)} %copy-done.2, f32[80,2560]{1,0:T(8,128)S(1)} %copy-done.3), kind=kLoop, calls=%fused_computation.2 | loop fusion | flops 3276800 | bytes 5734404 | tf_op jit(solution)/shard_map/sub | solution.py:427
  100.2 0.0 copy-done.1
  100.2 1.5 %copy.10 = bf16[512,2560]{1,0:T(8,128)(2,1)} copy(bf16[512,2560]{1,0:T(8,128)(2,1)S(1)} %copy-done.1) | data formatting | bytes 5242880
Async XLA Ops:
  0.6 96.4 %copy-start = (f32[80,2560]{1,0:T(8,128)S(1)}, f32[80,2560]{1,0:T(8,128)}, u32[]{:S(2)}) copy-start(f32[80,2560]{1,0:T(8,128)} %master_hbm.1) | copy-start | bytes 2457604
  0.6 96.4 %copy-start.3 = (f32[80,2560]{1,0:T(8,128)S(1)}, f32[80,2560]{1,0:T(8,128)}, u32[]{:S(2)}) copy-start(f32[80,2560]{1,0:T(8,128)} %param.9) | copy-start | bytes 2457604
  0.7 96.4 %copy-start.2 = (f32[80,2560]{1,0:T(8,128)S(1)}, f32[80,2560]{1,0:T(8,128)}, u32[]{:S(2)}) copy-start(f32[80,2560]{1,0:T(8,128)} %param.8) | copy-start | bytes 2457604
  97.0 3.2 %copy-start.1 = (bf16[512,2560]{1,0:T(8,128)(2,1)S(1)}, bf16[512,2560]{1,0:T(8,128)(2,1)}, u32[]{:S(2)}) copy-start(bf16[512,2560]{1,0:T(8,128)(2,1)} %get-tuple-element.17) | copy-start | bytes 7864324

commit v2 on v1

--- a/solution.py
+++ b/solution.py
@@ -13,9 +13,21 @@
 BF16 = jnp.bfloat16
 
 
-def kernel(nb, attn_hbm, og_hbm, master_hbm, ig_hbm, gw_ref, sq_ref,
-           attn_ref, og_ref, mst, rx_og, tbuf, tx, at_own, at_rx, wg, g, rx1, rzb, rx3, fbuf, ig, sqs,
-           l_s, o_s, x_s, x_r, p_s, p_r, z_s, z_r, e_s, e_r, c_s, c_r, r_s, r_r, y_s, y_r, f_s, f_r, q_s, q_r):
+def update(weight_grad, squares, master, moment_one, moment_two, size):
+    grad_norm = jnp.sqrt(squares) + 1e-06
+    limit = jnp.sqrt(jnp.float32(size))
+    clipped = weight_grad * jnp.minimum(jnp.float32(1.0), limit / grad_norm)
+    new_one = 0.9 * moment_one + 0.1 * clipped
+    new_two = 0.999 * moment_two + 0.001 * clipped * clipped
+    first_hat = new_one * (1.0 / (1.0 - 0.9**STEP))
+    second_hat = new_two * (1.0 / (1.0 - 0.999**STEP))
+    new_master = master - 0.01 * (first_hat / (jnp.sqrt(second_hat) + 1e-08) + 0.1 * master)
+    return new_master, new_one, new_two
+
+
+def kernel(nb, attn_hbm, og_hbm, master_hbm, m1_hbm, m2_hbm, ig, gw_ref, sq_ref, mst, m1, m2,
+           attn_ref, og_ref, rx_og, tbuf, tx, at_own, at_rx, wg, g, rx1, rzb, rx3, fbuf, sqs,
+           l_s, x_s, x_r, p_s, p_r, z_s, z_r, e_s, e_r, c_s, c_r, r_s, r_r, y_s, y_r, f_s, f_r, q_s, q_r):
     ns = 4
     nz = nb // 2
     tok, din = attn_ref.shape
@@ -48,13 +60,22 @@
     la.start()
     lg = pltpu.make_async_copy(og_hbm, og_ref, l_s.at[1])
     lg.start()
+    l1 = pltpu.make_async_copy(m1_hbm, m1, l_s.at[3])
+    l1.start()
+    l2 = pltpu.make_async_copy(m2_hbm, m2, l_s.at[4])
+    l2.start()
     barrier = pltpu.get_barrier_semaphore()
 
-    def greet(i, carry):
-        pl.semaphore_signal(barrier, inc=1, device_id=other(i), device_id_type=MESH)
-        return carry
-
-    lax.fori_loop(1, ns * nb, greet, 0)
+    def greet(s, b):
+        pl.semaphore_signal(barrier, inc=1, device_id=(s, b), device_id_type=MESH)
+
+    greet(sl, batch)
+    greet(sh, batch)
+    greet(*core_dev)
+    for step, ok in ((-2, z > 0), (2, z < nz - 1)):
+        @pl.when(ok)
+        def _():
+            greet(seq, batch + step)
 
     near = jnp.minimum(z, nz - 1 - z)
 
@@ -135,7 +156,8 @@
     def az(t, h, i):
         z_copy(h, i, t, 0).wait_recv()
         z_each(h, i, t, lambda c: c.start())
-        e_copy(h, i, t).start()
+        if t < nz - 1 or i == 0:
+            e_copy(h, i, t).start()
         if i == 1:
             c_copy(1 + h, t).start()
         elif h == 1:
@@ -186,6 +208,8 @@
             f_copy(h).start()
 
     tile = 256
+    far_cols = (nz - 1) * 2 * r // 128 * 128
+    near_cols = far_cols // (nz - 1)
 
     def grad(j):
         rows = pl.ds(pl.multiple_of(zk(nz - 1 - j) * (ns * r), 16), ns * r)
@@ -198,10 +222,11 @@
             return carry
         lax.fori_loop(0, dout // tile, body, 0)
 
-    def input_cols(q, s):
-        def part(c):
-            v = lax.dot_general(og_ref[...], wg[c, :], (((1,), (1,)), ((), ())), preferred_element_type=F32)
-            ig[:, c] = v.astype(BF16)
+    def part(c):
+        v = lax.dot_general(og_ref[...], wg[c, :], (((1,), (1,)), ((), ())), preferred_element_type=F32)
+        ig[:, c] = v.astype(BF16)
+
+    def input_cols(s):
 
         def body(i, carry):
             part(pl.ds(pl.multiple_of(s * block + i * tile, 128), tile))
@@ -209,18 +234,13 @@
         lax.fori_loop(0, block // tile, body, 0)
         if block % tile:
             part(pl.ds(pl.multiple_of(s * block + block // tile * tile, 128), block % tile))
-        o_copy(q, s).start()
-
-    def o_copy(q, s):
-        c = pl.ds(pl.multiple_of(s * block, 128), block)
-        return pltpu.make_async_copy(ig.at[:, c], ig_hbm.at[:, c], o_s.at[q])
 
     xo = remote(og_hbm, rx_og, x_s.at[0], x_r.at[0], core_dev)
     xt = remote(tx, at_rx, x_s.at[1], x_r.at[1], core_dev)
 
     lm.wait()
     wg[wrows(seq, z), :] = mst[...].astype(BF16)
-    pl.semaphore_wait(barrier, ns * nb - 1)
+    pl.semaphore_wait(barrier, 5 - edge.astype(jnp.int32))
     for h in (0, 1):
         p_copy(h).start()
     for h in (0, 1):
@@ -283,30 +303,34 @@
     for t in range(nz):
         c_copy(0, t).wait_recv()
     do([], [(rr, j, h, i) for h, i in ih[2:] for j in (1, 2)])
-    input_cols(0, seq)
+    input_cols(seq)
     do([(rr, 2, h, i) for h, i in ih], [])
-    for i in hs:
-        for h in hs:
-            ae(3, h, i)
-    for k in range(1, 7):
+    for h in hs:
+        ae(3, h, 0)
+    for h in hs:
+        rl(h, 1)
+    for h in hs:
+        e_copy(h, 1, nz - 1).start()
+    for k in (1, 2, 3, 5):
         for t in range(nz):
             c_copy(k, t).wait_recv()
-    input_cols(1, sl)
-    input_cols(2, sh)
-    rl(0, 1)
-    rl(1, 1)
-    input_cols(3, sd)
-    rl(0, 0)
-    rl(1, 0)
+    input_cols(sl)
+    input_cols(sh)
+    for k in (4, 6):
+        for t in range(nz - 1):
+            c_copy(k, t).wait_recv()
+    for h in hs:
+        rl(h, 0)
+    part(pl.ds(pl.multiple_of(sd * block + jnp.where(zk(nz - 1) == 0, block - far_cols, 0), 128), far_cols))
     for h in hs:
         f_copy(h).wait_recv()
         gw_ref[:, cols[h]] += rx3[h].astype(F32)
 
     v = gw_ref[...]
-    part = jnp.sum((v * v).reshape(r // 8, 8, dout), axis=0)
-    acc = part[:, :128]
+    fold = jnp.sum((v * v).reshape(r // 8, 8, dout), axis=0)
+    acc = fold[:, :128]
     for i in range(1, dout // 128):
-        acc += part[:, i * 128:(i + 1) * 128]
+        acc += fold[:, i * 128:(i + 1) * 128]
     sqs[0] = jnp.sum(acc, axis=0, keepdims=True)
 
     def q_copy(i):
@@ -321,6 +345,8 @@
         return carry
 
     lax.fori_loop(1, ns * nb, q_start, 0)
+    for h in hs:
+        ae(3, h, 1)
     for h in hs:
         p_copy(h).wait_send()
         f_copy(h).wait_send()
@@ -331,13 +357,16 @@
                 r_copy(h, i, t).wait_send()
                 if t < nz - 1:
                     y_copy(h, i, t).wait_send()
+    xo.wait_send()
+    xt.wait_send()
+    for k in (4, 6):
+        c_copy(k, nz - 1).wait_recv()
+    part(pl.ds(pl.multiple_of(sd * block + zk(nz - 1) * near_cols, 128), block - far_cols))
     for t in range(nz):
         for k in range(7):
             c_copy(k, t).wait_send()
-    xo.wait_send()
-    xt.wait_send()
-    for q, s in enumerate((seq, sl, sh, sd)):
-        o_copy(q, s).wait()
+    l1.wait()
+    l2.wait()
     lax.fori_loop(1, ns * nb, q_wait, 0)
     total = sqs[0]
     for i in range(1, ns * nb):
@@ -345,7 +374,36 @@
     sq_ref[...] = total
 
 
-def fused(attn_out, out_grad, master, ns, nb):
+def finish(size, ig, gw, sq, mst, m1, m2, ig_hbm, nm_hbm, n1_hbm, n2_hbm, nm, n1, n2, i_s, o_s):
+    ci = pltpu.make_async_copy(ig, ig_hbm, i_s.at[0])
+    ci.start()
+    steps = gw.shape[0] // 8
+    squares = jnp.sum(sq[...], axis=1, keepdims=True)
+
+    def copies(i):
+        rows = pl.ds(pl.multiple_of(i * 8, 8), 8)
+        return [pltpu.make_async_copy(a.at[rows], b.at[rows], o_s.at[k, i])
+                for k, (a, b) in enumerate(((nm, nm_hbm), (n1, n1_hbm), (n2, n2_hbm)))]
+
+    def body(i, carry):
+        rows = pl.ds(pl.multiple_of(i * 8, 8), 8)
+        nm[rows, :], n1[rows, :], n2[rows, :] = update(
+            gw[rows, :], squares, mst[rows, :], m1[rows, :], m2[rows, :], size)
+        for c in copies(i):
+            c.start()
+        return carry
+
+    def drain(i, carry):
+        for c in copies(i):
+            c.wait()
+        return carry
+
+    lax.fori_loop(0, steps, body, 0)
+    lax.fori_loop(0, steps, drain, 0)
+    ci.wait()
+
+
+def fused(attn_out, out_grad, master, moment_one, moment_two, ns, nb):
     tok, din = attn_out.shape
     dout = out_grad.shape[1]
     r = master.shape[0]
@@ -355,21 +413,17 @@
     dma = lambda k: pltpu.SemaphoreType.DMA((k,))
     vm = pl.BlockSpec(memory_space=pltpu.VMEM)
     hbm = pl.BlockSpec(memory_space=pl.ANY)
-    sems = [3, 4, 2, 2, 2, 2, 8 * nz, 4 * nz, 4 * nz, 4 * nz, 7 * nz, 7 * nz,
+    sems = [5, 2, 2, 2, 2, 8 * nz, 4 * nz, 4 * nz, 4 * nz, 7 * nz, 7 * nz,
             4 * nz, 4 * nz, 4 * nz, 4 * (nz + 1), 2, 2, n, n]
-    return pl.pallas_call(
+    flat = (r, dout), F32
+    held = pl.pallas_call(
         functools.partial(kernel, nb),
-        out_shape=(
-            jax.ShapeDtypeStruct((tok, din), BF16),
-            jax.ShapeDtypeStruct((r, dout), F32),
-            jax.ShapeDtypeStruct((1, 128), F32),
-        ),
-        in_specs=[hbm] * 3,
-        out_specs=(hbm, vm, vm),
+        out_shape=tuple(pltpu.VMEM(*o) for o in (((tok, din), BF16), flat, ((1, 128), F32), flat, flat, flat)),
+        in_specs=[hbm] * 5,
+        out_specs=(vm,) * 6,
         scratch_shapes=[
             pltpu.VMEM((tok, din), BF16),
             pltpu.VMEM((tok, dout), BF16),
-            pltpu.VMEM((r, dout), F32),
             pltpu.VMEM((tok, dout), BF16),
             pltpu.VMEM((nb * r, tok), BF16),
             pltpu.VMEM((din // 2, tok), BF16),
@@ -381,12 +435,19 @@
             pltpu.VMEM((4 * (nz + 1), r, half), BF16),
             pltpu.VMEM((2, r, half), BF16),
             pltpu.VMEM((2, r, half), F32),
-            pltpu.VMEM((tok, din), BF16),
             pltpu.VMEM((n, 1, 128), F32),
         ] + [dma(k) for k in sems],
         compiler_params=pltpu.CompilerParams(
-            collective_id=0, has_side_effects=True, vmem_limit_bytes=62_000_000),
-    )(attn_out, out_grad, master)
+            collective_id=0, has_side_effects=True, vmem_limit_bytes=52_000_000),
+    )(attn_out, out_grad, master, moment_one, moment_two)
+    return pl.pallas_call(
+        functools.partial(finish, din * dout),
+        out_shape=(jax.ShapeDtypeStruct((tok, din), BF16),) + (jax.ShapeDtypeStruct(*flat),) * 3,
+        in_specs=[vm] * 6,
+        out_specs=(hbm,) * 4,
+        scratch_shapes=[pltpu.VMEM(*flat)] * 3 + [dma(1), pltpu.SemaphoreType.DMA((3, r // 8))],
+        compiler_params=pltpu.CompilerParams(vmem_limit_bytes=6_000_000),
+    )(*(pltpu.with_memory_space_constraint(v, pltpu.VMEM) for v in held))
 
 
 def plain(attn_out, out_grad, shard_weight):
@@ -413,19 +474,9 @@
     r, dout = master.shape
     din = attn_out.shape[1]
     if ns == 4 and nb == 8 and r % 16 == 0 and (nb * r) % 128 == 0 and dout % 256 == 0:
-        input_grad, weight_grad, sq = fused(attn_out, out_grad, master, ns, nb)
-        squares = jnp.sum(sq)
-    else:
-        input_grad, weight_grad, squares = plain(attn_out, out_grad, master.astype(BF16))
-    grad_norm = jnp.sqrt(squares) + 1e-06
-    limit = jnp.sqrt(jnp.float32(din * dout))
-    clipped = weight_grad * jnp.minimum(jnp.float32(1.0), limit / grad_norm)
-    new_one = 0.9 * moment_one + 0.1 * clipped
-    new_two = 0.999 * moment_two + 0.001 * clipped * clipped
-    first_hat = new_one / (1.0 - 0.9**STEP)
-    second_hat = new_two / (1.0 - 0.999**STEP)
-    new_master = master - 0.01 * (first_hat / (jnp.sqrt(second_hat) + 1e-08) + 0.1 * master)
-    return (input_grad, new_master, new_one, new_two)
+        return fused(attn_out, out_grad, master, moment_one, moment_two, ns, nb)
+    input_grad, weight_grad, squares = plain(attn_out, out_grad, master.astype(BF16))
+    return (input_grad,) + update(weight_grad, squares, master, moment_one, moment_two, din * dout)
 
 
 def solution(mesh):

time: 102 us -> 93.2 us (0.914)
  other arithmetic: 4.42 us -> 0 us
  Pallas kernels: 94.3 us -> 92.2 us
  local copies, waits for them, and re-layouts: 1.51 us -> 0 us
    sub x1 -> x0, other arithmetic: 3.14 us -> none  [on_device(): master - 0.01 * (first_hat / (jnp.sqrt(second_hat) + 1e-08) + 0.1 * master)]
    pallas_call x1 -> x2, Pallas kernels: 94.3 us -> 92.2 us  [the longest x1 89.7 us: fused(): pl.pallas_call(functools.partial(kernel, nb), out_shape=tuple((pltpu.VMEM...]
    unnamed x9 -> x0, local copies, waits for them, and re-layouts: 1.51 us -> none
    reduce_sum x1 -> x0, other arithmetic: 1.28 us -> none  [on_device(): squares = jnp.sum(sq)]
where the time goes in v2:
time: 93.2 us; the launch traced here: 93 us
  Pallas kernels  92.2 us (99%)
    pallas_call x1, Pallas kernels, fused(): pl.pallas_call(functools.partial(kernel, nb), out_shape=tuple((pltpu.VMEM...  89.7 us
    pallas_call x1, Pallas kernels, fused(): pl.pallas_call(functools.partial(finish, din * dout), out_shape=(jax.Shap...  2.53 us

profile of v2, /device:TPU:0, one launch (start us, length us, event | category | flops | bytes accessed | tf_op | source)
XLA Modules:
  0.0 93.0 jit_solution(1572905344293662079)
XLA Ops:
  0.6 89.7 %shard_map.84 = (bf16[512,2560]{1,0:T(8,128)(2,1)S(1)}, f32[80,2560]{1,0:T(8,128)S(1)}, f32[1,128]{1,0:T(1,128)S(1)}, f32[80,2560]{1,0:T(8,128)S(1)}, f32[80,2560]{1,0:T(8,128)S(1)}, /*index=5*/f32[80,2560]{1,0:T(8,128)S(1)}) custom-call(bf16[512,2560]{1,0:T(8,128)(2,1)} %attn_hbm.1, bf16[512,2560]{1,0:T(8,128)(2,1)} %og_hbm.1, f32[80,2560]{1,0:T(8,128)} %master_hbm.1, ...), custom_call_target="tpu_custom_call" | custom-call | tf_op jit(solution)/shard_map/pallas_call | solution.py:419
  90.3 2.5 %shard_map.85 = (bf16[512,2560]{1,0:T(8,128)(2,1)}, f32[80,2560]{1,0:T(8,128)}, f32[80,2560]{1,0:T(8,128)}, f32[80,2560]{1,0:T(8,128)}) custom-call(bf16[512,2560]{1,0:T(8,128)(2,1)S(1)} %get-tuple-element.10.ig, f32[80,2560]{1,0:T(8,128)S(1)} %get-tuple-element.11.gw, f32[1,128]{1,0:T(1,128)S(1)} %get-tuple-element.12.sq, ...), custom_call_target="tpu_custom_call" | custom-call | tf_op jit(solution)/shard_map/pallas_call | solution.py:443

commit v3 on v2

--- a/solution.py
+++ b/solution.py
@@ -103,14 +103,14 @@
 
     def p_copy(h):
         v = shard(seq, z, h)
-        return remote(v, v, p_s.at[h], p_r.at[h], (first[h], batch))
+        return remote(v, v, p_s.at[0], p_r.at[h], (first[h], batch))
 
     def z_copy(h, i, t, up):
         zz = zk(t)
         to = jnp.minimum(z + 1, nz - 1) if up else jnp.maximum(z - 1, 0)
         v = shard((seq, first[h])[i], zz, h)
         k = (h * 2 + i) * nz + zz
-        return remote(v, v, z_s.at[4 * nz * up + k], z_r.at[k], (seq, to * 2 + core))
+        return remote(v, v, z_s.at[up], z_r.at[k], (seq, to * 2 + core))
 
     def z_each(h, i, t, act):
         zz = zk(t)
@@ -124,17 +124,22 @@
     def e_copy(h, i, t):
         v = shard((seq, first[h])[i], zk(t), h)
         k = (h * 2 + i) * nz + t
-        return remote(v, v, e_s.at[k], e_r.at[k], (last[h], batch))
+        return remote(v, v, e_s.at[0], e_r.at[k], (last[h], batch))
 
     def c_copy(k, t):
         s, h = ((seq, None), (sl, 0), (sh, 1), (sh, 0), (sd, 0), (sl, 1), (sd, 1))[k]
         v = wg.at[wrows(s, zk(t))] if h is None else shard(s, zk(t), h)
-        return remote(v, v, c_s.at[7 * t + k], c_r.at[7 * t + k], core_dev)
+        return remote(v, v, c_s.at[0], c_r.at[c_group(k, t)], core_dev)
+
+    def c_group(k, t):
+        if k in (4, 6):
+            return 3 if t == nz - 1 else 2
+        return 1 if k else 0
 
     def r_copy(h, i, j):
         k = (h * 2 + i) * nz + j
         v = g.at[grows((last[h], sd)[i], zk(nz - 1 - j)), cols[h]]
-        return remote(v, rx1.at[k], r_s.at[k], r_r.at[k], (last[h], batch))
+        return remote(v, rx1.at[k], r_s.at[0], r_r.at[k], (last[h], batch))
 
     def y_copy(h, i, j):
         t = zk(nz - 1 - j)
@@ -142,7 +147,7 @@
         to = jnp.where(up, jnp.minimum(z + 1, nz - 1), jnp.maximum(z - 1, 0))
         k = (h * 2 + i) * (nz + 1) + jnp.where(jnp.logical_and(jnp.logical_not(up), t == z - 1), nz, t)
         v = g.at[grows((seq, first[h])[i], t), cols[h]]
-        return remote(v, rzb.at[k], y_s.at[(h * 2 + i) * nz + j], y_r.at[k], (seq, to * 2 + core))
+        return remote(v, rzb.at[k], y_s.at[0], y_r.at[k], (seq, to * 2 + core))
 
     def y_slot(h, i, t):
         k = (h * 2 + i) * (nz + 1) + t
@@ -151,7 +156,14 @@
 
     def f_copy(h):
         v = g.at[grows(first[h], z), cols[h]]
-        return remote(v, rx3.at[h], f_s.at[h], f_r.at[h], (first[h], batch))
+        return remote(v, rx3.at[h], f_s.at[0], f_r.at[h], (first[h], batch))
+
+    def all_of(ref, ssem, rsem):
+        return remote(ref, ref, ssem, rsem, core_dev)
+
+    def c_wait(group):
+        rows = (nz * r, 4 * nz * r // 2, 6 * (nz - 1) * r // 6, r)[group]
+        all_of(wg.at[pl.ds(0, rows)], c_s.at[0], c_r.at[group]).wait_recv()
 
     def az(t, h, i):
         z_copy(h, i, t, 0).wait_recv()
@@ -300,8 +312,7 @@
        + [(rs, 3)]
        + [(ae, t, h, i) for t in (0, 1, 2) for i in hs for h in hs]
        + [(rr, j, h, i) for h, i in ih[:2] for j in (1, 2)])
-    for t in range(nz):
-        c_copy(0, t).wait_recv()
+    c_wait(0)
     do([], [(rr, j, h, i) for h, i in ih[2:] for j in (1, 2)])
     input_cols(seq)
     do([(rr, 2, h, i) for h, i in ih], [])
@@ -311,14 +322,10 @@
         rl(h, 1)
     for h in hs:
         e_copy(h, 1, nz - 1).start()
-    for k in (1, 2, 3, 5):
-        for t in range(nz):
-            c_copy(k, t).wait_recv()
+    c_wait(1)
     input_cols(sl)
     input_cols(sh)
-    for k in (4, 6):
-        for t in range(nz - 1):
-            c_copy(k, t).wait_recv()
+    c_wait(2)
     for h in hs:
         rl(h, 0)
     part(pl.ds(pl.multiple_of(sd * block + jnp.where(zk(nz - 1) == 0, block - far_cols, 0), 128), far_cols))
@@ -334,40 +341,32 @@
     sqs[0] = jnp.sum(acc, axis=0, keepdims=True)
 
     def q_copy(i):
-        return remote(sqs.at[0], sqs.at[i], q_s.at[i], q_r.at[i], other(i))
+        return remote(sqs.at[0], sqs.at[i], q_s.at[0], q_r.at[0], other(i))
 
     def q_start(i, carry):
         q_copy(i).start()
         return carry
 
-    def q_wait(i, carry):
-        q_copy(i).wait()
-        return carry
-
     lax.fori_loop(1, ns * nb, q_start, 0)
     for h in hs:
         ae(3, h, 1)
-    for h in hs:
-        p_copy(h).wait_send()
-        f_copy(h).wait_send()
-        for i in hs:
-            for t in range(nz):
-                z_each(h, i, t, lambda c: c.wait_send())
-                e_copy(h, i, t).wait_send()
-                r_copy(h, i, t).wait_send()
-                if t < nz - 1:
-                    y_copy(h, i, t).wait_send()
     xo.wait_send()
     xt.wait_send()
-    for k in (4, 6):
-        c_copy(k, nz - 1).wait_recv()
+    c_wait(3)
     part(pl.ds(pl.multiple_of(sd * block + zk(nz - 1) * near_cols, 128), block - far_cols))
-    for t in range(nz):
-        for k in range(7):
-            c_copy(k, t).wait_send()
+    for n, sem in ((2, p_s), (2, f_s), (4 * nz, e_s), (4 * nz, r_s), (4 * (nz - 1), y_s)):
+        all_of(rx1.at[pl.ds(0, n)], sem.at[0], q_r.at[0]).wait_send()
+    for k in range(nz):
+        @pl.when(z == k)
+        def _():
+            if k < nz - 1:
+                all_of(rx1.at[pl.ds(0, 4 * (k + 1))], z_s.at[1], q_r.at[0]).wait_send()
+            if k:
+                all_of(rx1.at[pl.ds(0, 4 * (nz - k))], z_s.at[0], q_r.at[0]).wait_send()
+    all_of(wg.at[pl.ds(0, 4 * nz * r)], c_s.at[0], q_r.at[0]).wait_send()
     l1.wait()
     l2.wait()
-    lax.fori_loop(1, ns * nb, q_wait, 0)
+    all_of(sqs.at[pl.ds(1, ns * nb - 1)], q_s.at[0], q_r.at[0]).wait()
     total = sqs[0]
     for i in range(1, ns * nb):
         total += sqs[i]
@@ -413,8 +412,7 @@
     dma = lambda k: pltpu.SemaphoreType.DMA((k,))
     vm = pl.BlockSpec(memory_space=pltpu.VMEM)
     hbm = pl.BlockSpec(memory_space=pl.ANY)
-    sems = [5, 2, 2, 2, 2, 8 * nz, 4 * nz, 4 * nz, 4 * nz, 7 * nz, 7 * nz,
-            4 * nz, 4 * nz, 4 * nz, 4 * (nz + 1), 2, 2, n, n]
+    sems = [5, 2, 2, 1, 2, 2, 4 * nz, 1, 4 * nz, 1, 4, 1, 4 * nz, 1, 4 * (nz + 1), 1, 2, 1, 1]
     flat = (r, dout), F32
     held = pl.pallas_call(
         functools.partial(kernel, nb),

time: 93.2 us -> 91.2 us (0.979)
  Pallas kernels: 92.2 us -> 90.4 us
    pallas_call x1, Pallas kernels: 89.7 us -> 87.9 us  [fused(): pl.pallas_call(functools.partial(kernel, nb), out_shape=tuple((pltpu.VMEM...]
where the time goes in v3:
time: 91.2 us; the launch traced here: 91 us
  Pallas kernels  90.4 us (99%)
    pallas_call x1, Pallas kernels, fused(): pl.pallas_call(functools.partial(kernel, nb), out_shape=tuple((pltpu.VMEM...  87.9 us
    pallas_call x1, Pallas kernels, fused(): pl.pallas_call(functools.partial(finish, din * dout), out_shape=(jax.Shap...  2.53 us

profile of v3, /device:TPU:0, one launch (start us, length us, event | category | flops | bytes accessed | tf_op | source)
XLA Modules:
  0.0 91.0 jit_solution(13245408858558107972)
XLA Ops:
  0.6 87.9 %shard_map.84 = (bf16[512,2560]{1,0:T(8,128)(2,1)S(1)}, f32[80,2560]{1,0:T(8,128)S(1)}, f32[1,128]{1,0:T(1,128)S(1)}, f32[80,2560]{1,0:T(8,128)S(1)}, f32[80,2560]{1,0:T(8,128)S(1)}, /*index=5*/f32[80,2560]{1,0:T(8,128)S(1)}) custom-call(bf16[512,2560]{1,0:T(8,128)(2,1)} %attn_hbm.1, bf16[512,2560]{1,0:T(8,128)(2,1)} %og_hbm.1, f32[80,2560]{1,0:T(8,128)} %master_hbm.1, ...), custom_call_target="tpu_custom_call" | custom-call | tf_op jit(solution)/shard_map/pallas_call | solution.py:417
  88.5 2.5 %shard_map.85 = (bf16[512,2560]{1,0:T(8,128)(2,1)}, f32[80,2560]{1,0:T(8,128)}, f32[80,2560]{1,0:T(8,128)}, f32[80,2560]{1,0:T(8,128)}) custom-call(bf16[512,2560]{1,0:T(8,128)(2,1)S(1)} %get-tuple-element.10.ig, f32[80,2560]{1,0:T(8,128)S(1)} %get-tuple-element.11.gw, f32[1,128]{1,0:T(1,128)S(1)} %get-tuple-element.12.sq, ...), custom_call_target="tpu_custom_call" | custom-call | tf_op jit(solution)/shard_map/pallas_call | solution.py:441

commit v4 on v3

--- a/solution.py
+++ b/solution.py
@@ -25,15 +25,22 @@
     return new_master, new_one, new_two
 
 
+def widths(dout):
+    tiles = dout // 128 - 1
+    wide = (tiles + 1) // 2 * 128
+    return wide, tiles * 128 - wide, tiles * 128
+
+
 def kernel(nb, attn_hbm, og_hbm, master_hbm, m1_hbm, m2_hbm, ig, gw_ref, sq_ref, mst, m1, m2,
            attn_ref, og_ref, rx_og, tbuf, tx, at_own, at_rx, wg, g, rx1, rzb, rx3, fbuf, sqs,
-           l_s, x_s, x_r, p_s, p_r, z_s, z_r, e_s, e_r, c_s, c_r, r_s, r_r, y_s, y_r, f_s, f_r, q_s, q_r):
+           tz, ty, tl, tsum,
+           l_s, x_s, x_r, p_s, p_r, z_s, z_r, e_s, e_r, c_s, c_r, r_s, r_r, y_s, y_r, f_s, f_r, q_s, q_r,
+           a_s, a_r, b_s, b_r, d_s, d_r, t_s, t_r, u_s, u_r):
     ns = 4
     nz = nb // 2
     tok, din = attn_ref.shape
     dout = og_ref.shape[1]
     r = gw_ref.shape[0]
-    half = dout // 2
     block = nb * r
     seq = lax.axis_index("seq")
     batch = lax.axis_index("batch")
@@ -46,7 +53,12 @@
     sd = (1 - hi) * 2 + (1 - lo)
     first = (sl, sh)
     last = (sh, sl)
-    cols = (pl.ds(0, half), pl.ds(half, half))
+    wide, slim, both = widths(dout)
+    gcols = (pl.ds(0, wide), pl.ds(wide, slim))
+    rcols = (pl.ds(0, slim), pl.ds(slim, wide))
+    rw = (pl.ds(0, slim), pl.ds(0, wide))
+    bcols = pl.ds(0, both)
+    tcols = pl.ds(both, dout - both)
     core_dev = (seq, z * 2 + 1 - core)
     edge = jnp.logical_or(z == 0, z == nz - 1)
 
@@ -87,8 +99,8 @@
         above = jnp.where(both, t % 2, jnp.where(z < nz - 1 - z, 1, 0))
         return z + dist * (2 * above - 1)
 
-    def wrows(s, zz):
-        return pl.ds(pl.multiple_of((s * nb + zz * 2 + core) * r, 16), r)
+    def wrows(zz):
+        return pl.ds(pl.multiple_of((zz * 2 + core) * r, 16), r)
 
     def grows(s, zz):
         return pl.ds(pl.multiple_of((zz * ns + s) * r, 16), r)
@@ -99,7 +111,7 @@
             device_id=dev, device_id_type=MESH)
 
     def shard(s, zz, h):
-        return wg.at[wrows(s, zz), cols[h]]
+        return wg.at[s, wrows(zz), gcols[h]]
 
     def p_copy(h):
         v = shard(seq, z, h)
@@ -128,42 +140,121 @@
 
     def c_copy(k, t):
         s, h = ((seq, None), (sl, 0), (sh, 1), (sh, 0), (sd, 0), (sl, 1), (sd, 1))[k]
-        v = wg.at[wrows(s, zk(t))] if h is None else shard(s, zk(t), h)
+        v = wg.at[s, wrows(zk(t)), bcols] if h is None else shard(s, zk(t), h)
         return remote(v, v, c_s.at[0], c_r.at[c_group(k, t)], core_dev)
 
     def c_group(k, t):
-        if k in (4, 6):
-            return 3 if t == nz - 1 else 2
-        return 1 if k else 0
+        if t < nz - 1:
+            return 0
+        return 3 if k in (4, 6) else 2 if k else 1
 
     def r_copy(h, i, j):
         k = (h * 2 + i) * nz + j
-        v = g.at[grows((last[h], sd)[i], zk(nz - 1 - j)), cols[h]]
-        return remote(v, rx1.at[k], r_s.at[0], r_r.at[k], (last[h], batch))
+        v = g.at[grows((last[h], sd)[i], zk(nz - 1 - j)), rcols[h]]
+        return remote(v, rx1.at[k, :, rw[h]], r_s.at[0], r_r.at[k], (last[h], batch))
 
     def y_copy(h, i, j):
         t = zk(nz - 1 - j)
         up = t > z
         to = jnp.where(up, jnp.minimum(z + 1, nz - 1), jnp.maximum(z - 1, 0))
         k = (h * 2 + i) * (nz + 1) + jnp.where(jnp.logical_and(jnp.logical_not(up), t == z - 1), nz, t)
-        v = g.at[grows((seq, first[h])[i], t), cols[h]]
-        return remote(v, rzb.at[k], y_s.at[0], y_r.at[k], (seq, to * 2 + core))
+        v = g.at[grows((seq, first[h])[i], t), rcols[h]]
+        return remote(v, rzb.at[k, :, rw[h]], y_s.at[0], y_r.at[k], (seq, to * 2 + core))
 
     def y_slot(h, i, t):
         k = (h * 2 + i) * (nz + 1) + t
-        v = g.at[grows(seq, z), cols[h]]
-        return remote(v, rzb.at[k], y_s.at[0], y_r.at[k], core_dev), rzb.at[k]
+        v = rzb.at[k, :, rw[h]]
+        return remote(v, v, y_s.at[0], y_r.at[k], core_dev), v
 
     def f_copy(h):
-        v = g.at[grows(first[h], z), cols[h]]
-        return remote(v, rx3.at[h], f_s.at[0], f_r.at[h], (first[h], batch))
+        v = g.at[grows(first[h], z), rcols[h]]
+        return remote(v, rx3.at[h, :, rw[h]], f_s.at[0], f_r.at[h], (first[h], batch))
 
     def all_of(ref, ssem, rsem):
         return remote(ref, ref, ssem, rsem, core_dev)
 
     def c_wait(group):
-        rows = (nz * r, 4 * nz * r // 2, 6 * (nz - 1) * r // 6, r)[group]
-        all_of(wg.at[pl.ds(0, rows)], c_s.at[0], c_r.at[group]).wait_recv()
+        v = (wg.at[pl.ds(0, nz - 1), pl.ds(0, ns * r), bcols] if group == 0
+             else wg.at[0, pl.ds(0, (1, 2, 1)[group - 1] * r), bcols])
+        all_of(v, c_s.at[0], c_r.at[group]).wait_recv()
+
+    def d_wait(group):
+        v = wg.at[:, pl.ds(0, (nz - 1, 1)[group] * r), tcols]
+        all_of(v, d_s.at[0], d_r.at[group]).wait_recv()
+
+    def a_copy(k):
+        s, to = ((seq, sh), (seq, sl), (sh, sl))[k]
+        v = wg.at[s, wrows(z), tcols]
+        return remote(v, v, a_s.at[0], a_r.at[k], (to, batch))
+
+    def b_copy(t, up):
+        to = jnp.minimum(z + 1, nz - 1) if up else jnp.maximum(z - 1, 0)
+        v = wg.at[:, wrows(zk(t)), tcols]
+        return remote(v, v, b_s.at[up], b_r.at[zk(t)], (seq, to * 2 + core))
+
+    def b_each(t, act):
+        zz = zk(t)
+        for up in (0, 1):
+            ok = jnp.logical_and(zz <= z, z < nz - 1) if up else jnp.logical_and(zz >= z, z > 0)
+
+            @pl.when(ok)
+            def _():
+                act(b_copy(t, up))
+
+    def d_copy(t):
+        v = wg.at[:, wrows(zk(t)), tcols]
+        return remote(v, v, d_s.at[0], d_r.at[t // (nz - 1)], core_dev)
+
+    def ab(t):
+        b_copy(t, 0).wait_recv()
+        b_each(t, lambda c: c.start())
+        d_copy(t).start()
+
+    def trows(t):
+        return pl.ds(pl.multiple_of(t * (ns * r), 16), ns * r)
+
+    def t_copy(j):
+        t = zk(nz - 1 - j)
+        up = t > z
+        to = jnp.where(up, jnp.minimum(z + 1, nz - 1), jnp.maximum(z - 1, 0))
+        k = jnp.where(jnp.logical_and(jnp.logical_not(up), t == z - 1), nz, t)
+        return remote(g.at[trows(t), tcols], tz.at[k], t_s.at[0], t_r.at[k], (seq, to * 2 + core))
+
+    def tr(j):
+        t = zk(nz - 1 - j)
+        more = jnp.logical_or(jnp.logical_and(t > z, z > 0), jnp.logical_and(t < z, z < nz - 1))
+
+        @pl.when(more)
+        def _():
+            all_of(tz.at[t], t_s.at[0], t_r.at[t]).wait_recv()
+            g[trows(t), tcols] = (g[trows(t), tcols].astype(F32) + tz[t].astype(F32)).astype(BF16)
+        t_copy(j).start()
+
+    def u_copy(k):
+        if k == 0:
+            v = g.at[pl.ds(pl.multiple_of(z * (ns * r) + (1 - hi) * (2 * r), 16), 2 * r), tcols]
+            return remote(v, ty, u_s.at[0], u_r.at[0], (sh, batch))
+        return remote(g.at[grows(sl, z), tcols], tl, u_s.at[1], u_r.at[1], (sl, batch))
+
+    def tl1():
+        tsum[...] = g[trows(z), tcols].astype(F32)
+        for ok, k in ((z > 0, z), (z < nz - 1, nz)):
+            @pl.when(ok)
+            def _():
+                all_of(tz.at[k], t_s.at[0], t_r.at[k]).wait_recv()
+                tsum[...] += tz[k].astype(F32)
+        away = pl.ds(pl.multiple_of((1 - hi) * (2 * r), 16), 2 * r)
+        g[pl.ds(pl.multiple_of(z * (ns * r) + (1 - hi) * (2 * r), 16), 2 * r), tcols] = tsum[away, :].astype(BF16)
+        u_copy(0).start()
+
+    def tl2():
+        u_copy(0).wait_recv()
+        mine = pl.ds(pl.multiple_of((hi * 2 + lo) * r, 16), r)
+        his = pl.ds(pl.multiple_of((hi * 2 + 1 - lo) * r, 16), r)
+        gw_ref[:, tcols] = tsum[mine, :] + ty[pl.ds(pl.multiple_of(lo * r, 16), r), :].astype(F32)
+        v = tsum[his, :] + ty[pl.ds(pl.multiple_of((1 - lo) * r, 16), r), :].astype(F32)
+        g[grows(sl, z), tcols] = v.astype(BF16)
+        u_copy(1).start()
 
     def az(t, h, i):
         z_copy(h, i, t, 0).wait_recv()
@@ -195,20 +286,21 @@
         def _():
             c, buf = y_slot(h, i, t)
             c.wait_recv()
-            g[rows, cols[h]] = (g[rows, cols[h]].astype(F32) + rx1[k].astype(F32) + buf[...].astype(F32)).astype(BF16)
+            g[rows, rcols[h]] = (g[rows, rcols[h]].astype(F32) + rx1[k, :, rw[h]].astype(F32)
+                                 + buf[...].astype(F32)).astype(BF16)
 
         @pl.when(jnp.logical_not(more))
         def _():
-            g[rows, cols[h]] = (g[rows, cols[h]].astype(F32) + rx1[k].astype(F32)).astype(BF16)
+            g[rows, rcols[h]] = (g[rows, rcols[h]].astype(F32) + rx1[k, :, rw[h]].astype(F32)).astype(BF16)
         y_copy(h, i, j).start()
 
     def rl(h, i):
         j = nz - 1
         k = (h * 2 + i) * nz + j
         rows = grows((seq, first[h])[i], z)
-        dst = gw_ref.at[:, cols[h]] if i == 0 else fbuf.at[h]
+        dst = gw_ref.at[:, rcols[h]] if i == 0 else fbuf.at[h, :, rw[h]]
         r_copy(h, i, j).wait_recv()
-        dst[...] = g[rows, cols[h]].astype(F32) + rx1[k].astype(F32)
+        dst[...] = g[rows, rcols[h]].astype(F32) + rx1[k, :, rw[h]].astype(F32)
         for ok, t in ((z > 0, z), (z < nz - 1, nz)):
             @pl.when(ok)
             def _():
@@ -216,7 +308,7 @@
                 c.wait_recv()
                 dst[...] += buf[...].astype(F32)
         if i == 1:
-            g[rows, cols[h]] = dst[...].astype(BF16)
+            g[rows, rcols[h]] = dst[...].astype(BF16)
             f_copy(h).start()
 
     tile = 256
@@ -234,31 +326,29 @@
             return carry
         lax.fori_loop(0, dout // tile, body, 0)
 
-    def part(c):
-        v = lax.dot_general(og_ref[...], wg[c, :], (((1,), (1,)), ((), ())), preferred_element_type=F32)
-        ig[:, c] = v.astype(BF16)
-
-    def input_cols(s):
-
-        def body(i, carry):
-            part(pl.ds(pl.multiple_of(s * block + i * tile, 128), tile))
-            return carry
-        lax.fori_loop(0, block // tile, body, 0)
-        if block % tile:
-            part(pl.ds(pl.multiple_of(s * block + block // tile * tile, 128), block % tile))
+    def part(s, c, n):
+        v = lax.dot_general(og_ref[...], wg[s, pl.ds(pl.multiple_of(c, 128), n), :], (((1,), (1,)), ((), ())),
+                            preferred_element_type=F32)
+        ig[:, pl.ds(pl.multiple_of(s * block + c, 128), n)] = v.astype(BF16)
+
+    def early(s):
+        part(s, jnp.where(zk(nz - 1) == 0, block - far_cols, 0), far_cols)
+
+    def late(s):
+        part(s, zk(nz - 1) * near_cols, block - far_cols)
 
     xo = remote(og_hbm, rx_og, x_s.at[0], x_r.at[0], core_dev)
     xt = remote(tx, at_rx, x_s.at[1], x_r.at[1], core_dev)
 
     lm.wait()
-    wg[wrows(seq, z), :] = mst[...].astype(BF16)
+    wg[seq, wrows(z), :] = mst[...].astype(BF16)
     pl.semaphore_wait(barrier, 5 - edge.astype(jnp.int32))
+    for k in (0, 1):
+        a_copy(k).start()
     for h in (0, 1):
         p_copy(h).start()
     for h in (0, 1):
         z_each(h, 0, 0, lambda c: c.start())
-    for h in (1, 0):
-        e_copy(h, 0, 0).start()
     xo.start()
     la.wait()
     for s in range(ns):
@@ -268,12 +358,20 @@
             at_own[rows, :] = tbuf[pl.ds(pl.multiple_of((zz * 2 + core) * r, 16), r), :]
             tx[rows, :] = tbuf[pl.ds(pl.multiple_of((zz * 2 + 1 - core) * r, 16), r), :]
     xt.start()
+    a_copy(0).wait_recv()
+    a_copy(2).start()
+    for h in (1, 0):
+        e_copy(h, 0, 0).start()
     c_copy(0, 0).start()
     for h in (0, 1):
         p_copy(h).wait_recv()
         z_each(h, 1, 0, lambda c: c.start())
         e_copy(h, 1, 0).start()
         c_copy(1 + h, 0).start()
+    for k in (1, 2):
+        a_copy(k).wait_recv()
+    b_each(0, lambda c: c.start())
+    d_copy(0).start()
     lg.wait()
     xo.wait_recv()
     xt.wait_recv()
@@ -290,48 +388,58 @@
     ih = [(h, i) for i in (1, 0) for h in hs]
     grad(0)
     rs(0)
-    do([(az, 1, h, 0) for h in hs],
+    do([(tr, 0)] + [(az, 1, h, 0) for h in hs],
        [(az, t, h, 0) for h in hs for t in (1, 2)])
     grad(1)
-    do([(az, 1, 0, 1)],
+    do([(tr, 1), (az, 1, 0, 1)],
        [(az, t, 0, 1) for t in (1, 2)])
     grad(2)
-    do([(az, 1, 1, 1), (rs, 1)],
+    do([(tr, 2), (az, 1, 1, 1), (rs, 1)],
        [(az, t, 1, 1) for t in (1, 2)] + [(rs, 1), (rs, 2)])
     do([(rr, 0, h, i) for h, i in ih[:2]], [])
     grad(3)
-    do([(rr, 0, h, i) for h, i in ih[2:]]
-       + [(az, 2, h, i) for i in hs for h in hs]
-       + [(rs, 2)]
-       + [(rr, 1, h, i) for h, i in ih]
+    do([(rr, 0, h, i) for h, i in ih[2:]] + [(ab, 1)]
+       + [(az, 2, h, 0) for h in hs] + [(rs, 2)] + [(az, 2, h, 1) for h in hs]
+       + [(rr, 1, h, i) for h, i in ih] + [(ab, 2)]
        + [(ae, t, h, i) for t in (0, 1) for i in hs for h in hs]
        + [(az, 3, h, i) for i in hs for h in hs]
-       + [(rs, 3)]
+       + [(rs, 3)] + [(rr, 2, h, i) for h, i in ih]
        + [(ae, 2, h, i) for i in hs for h in hs],
-       [e for n, (h, i) in enumerate(ih) for e in ((az, 3, n % 2, n // 2), (rr, 0, h, i))]
-       + [(rs, 3)]
+       [(ab, 1), (ab, 2), (tr, 0)]
+       + [e for n, (h, i) in enumerate(ih) for e in ((az, 3, n % 2, n // 2), (rr, 0, h, i))]
+       + [(tr, 1), (tr, 2), (rs, 3)]
        + [(ae, t, h, i) for t in (0, 1, 2) for i in hs for h in hs]
+       + [(ab, 3)]
        + [(rr, j, h, i) for h, i in ih[:2] for j in (1, 2)])
+    do([], [(rr, j, h, i) for h, i in ih[2:] for j in (1, 2)])
     c_wait(0)
-    do([], [(rr, j, h, i) for h, i in ih[2:] for j in (1, 2)])
-    input_cols(seq)
-    do([(rr, 2, h, i) for h, i in ih], [])
+    d_wait(0)
+    early(seq)
+    early(sl)
+    early(sh)
+    early(sd)
+    do([(ab, 3)], [])
+    tl1()
     for h in hs:
         ae(3, h, 0)
+    c_wait(1)
+    d_wait(1)
+    late(seq)
     for h in hs:
         rl(h, 1)
-    for h in hs:
-        e_copy(h, 1, nz - 1).start()
-    c_wait(1)
-    input_cols(sl)
-    input_cols(sh)
+    e_copy(0, 1, nz - 1).start()
+    tl2()
+    e_copy(1, 1, nz - 1).start()
     c_wait(2)
+    late(sl)
+    late(sh)
     for h in hs:
         rl(h, 0)
-    part(pl.ds(pl.multiple_of(sd * block + jnp.where(zk(nz - 1) == 0, block - far_cols, 0), 128), far_cols))
     for h in hs:
         f_copy(h).wait_recv()
-        gw_ref[:, cols[h]] += rx3[h].astype(F32)
+        gw_ref[:, rcols[h]] += rx3[h, :, rw[h]].astype(F32)
+    u_copy(1).wait_recv()
+    gw_ref[:, tcols] += tl[...].astype(F32)
 
     v = gw_ref[...]
     fold = jnp.sum((v * v).reshape(r // 8, 8, dout), axis=0)
@@ -353,17 +461,22 @@
     xo.wait_send()
     xt.wait_send()
     c_wait(3)
-    part(pl.ds(pl.multiple_of(sd * block + zk(nz - 1) * near_cols, 128), block - far_cols))
-    for n, sem in ((2, p_s), (2, f_s), (4 * nz, e_s), (4 * nz, r_s), (4 * (nz - 1), y_s)):
-        all_of(rx1.at[pl.ds(0, n)], sem.at[0], q_r.at[0]).wait_send()
+    late(sd)
+    for n, sem in ((1, p_s), (1, f_s), (2 * nz, e_s), (2 * nz, r_s), (2 * (nz - 1), y_s)):
+        all_of(wg.at[0, pl.ds(0, n * r), bcols], sem.at[0], q_r.at[0]).wait_send()
     for k in range(nz):
         @pl.when(z == k)
         def _():
-            if k < nz - 1:
-                all_of(rx1.at[pl.ds(0, 4 * (k + 1))], z_s.at[1], q_r.at[0]).wait_send()
-            if k:
-                all_of(rx1.at[pl.ds(0, 4 * (nz - k))], z_s.at[0], q_r.at[0]).wait_send()
-    all_of(wg.at[pl.ds(0, 4 * nz * r)], c_s.at[0], q_r.at[0]).wait_send()
+            for up, n in ((1, k + 1 if k < nz - 1 else 0), (0, nz - k if k else 0)):
+                if n:
+                    all_of(wg.at[0, pl.ds(0, 2 * n * r), bcols], z_s.at[up], q_r.at[0]).wait_send()
+                    all_of(wg.at[:, pl.ds(0, n * r), tcols], b_s.at[up], q_r.at[0]).wait_send()
+    all_of(wg.at[pl.ds(0, 2), :, bcols], c_s.at[0], q_r.at[0]).wait_send()
+    all_of(wg.at[:, pl.ds(0, nz * r), tcols], d_s.at[0], q_r.at[0]).wait_send()
+    all_of(tz.at[pl.ds(0, nz - 1)], t_s.at[0], q_r.at[0]).wait_send()
+    all_of(wg.at[pl.ds(0, 3), pl.ds(0, r), tcols], a_s.at[0], q_r.at[0]).wait_send()
+    for k in (0, 1):
+        u_copy(k).wait_send()
     l1.wait()
     l2.wait()
     all_of(sqs.at[pl.ds(1, ns * nb - 1)], q_s.at[0], q_r.at[0]).wait()
@@ -406,13 +519,15 @@
     tok, din = attn_out.shape
     dout = out_grad.shape[1]
     r = master.shape[0]
-    half = dout // 2
+    wide, _, both = widths(dout)
+    rest = dout - both
     nz = nb // 2
     n = ns * nb
     dma = lambda k: pltpu.SemaphoreType.DMA((k,))
     vm = pl.BlockSpec(memory_space=pltpu.VMEM)
     hbm = pl.BlockSpec(memory_space=pl.ANY)
-    sems = [5, 2, 2, 1, 2, 2, 4 * nz, 1, 4 * nz, 1, 4, 1, 4 * nz, 1, 4 * (nz + 1), 1, 2, 1, 1]
+    sems = [5, 2, 2, 1, 2, 2, 4 * nz, 1, 4 * nz, 1, 4, 1, 4 * nz, 1, 4 * (nz + 1), 1, 2, 1, 1,
+            1, 3, 2, nz, 1, 2, 1, nz + 1, 2, 2]
     flat = (r, dout), F32
     held = pl.pallas_call(
         functools.partial(kernel, nb),
@@ -427,13 +542,17 @@
             pltpu.VMEM((din // 2, tok), BF16),
             pltpu.VMEM((din // 2, tok), BF16),
             pltpu.VMEM((din // 2, tok), BF16),
-            pltpu.VMEM((din, dout), BF16),
+            pltpu.VMEM((ns, nb * r, dout), BF16),
             pltpu.VMEM((din // 2, dout), BF16),
-            pltpu.VMEM((4 * nz, r, half), BF16),
-            pltpu.VMEM((4 * (nz + 1), r, half), BF16),
-            pltpu.VMEM((2, r, half), BF16),
-            pltpu.VMEM((2, r, half), F32),
+            pltpu.VMEM((4 * nz, r, wide), BF16),
+            pltpu.VMEM((4 * (nz + 1), r, wide), BF16),
+            pltpu.VMEM((2, r, wide), BF16),
+            pltpu.VMEM((2, r, wide), F32),
             pltpu.VMEM((n, 1, 128), F32),
+            pltpu.VMEM((nz + 1, ns * r, rest), BF16),
+            pltpu.VMEM((2 * r, rest), BF16),
+            pltpu.VMEM((r, rest), BF16),
+            pltpu.VMEM((ns * r, rest), F32),
         ] + [dma(k) for k in sems],
         compiler_params=pltpu.CompilerParams(
             collective_id=0, has_side_effects=True, vmem_limit_bytes=52_000_000),

time: 91.2 us -> 89.6 us (0.982)
  Pallas kernels: 90.4 us -> 88.6 us
    pallas_call x1, Pallas kernels: 87.9 us -> 86.1 us  [fused(): pl.pallas_call(functools.partial(kernel, nb), out_shape=tuple((pltpu.VMEM...]
where the time goes in v4:
time: 89.6 us; the launch traced here: 89.4 us
  Pallas kernels  88.6 us (99%)
    pallas_call x1, Pallas kernels, fused(): pl.pallas_call(functools.partial(kernel, nb), out_shape=tuple((pltpu.VMEM...  86.1 us
    pallas_call x1, Pallas kernels, fused(): pl.pallas_call(functools.partial(finish, din * dout), out_shape=(jax.Shap...  2.53 us

profile of v4, /device:TPU:0, one launch (start us, length us, event | category | flops | bytes accessed | tf_op | source)
XLA Modules:
  0.0 89.4 jit_solution(6364184347167941049)
XLA Ops:
  0.6 86.1 %shard_map.84 = (bf16[512,2560]{1,0:T(8,128)(2,1)S(1)}, f32[80,2560]{1,0:T(8,128)S(1)}, f32[1,128]{1,0:T(1,128)S(1)}, f32[80,2560]{1,0:T(8,128)S(1)}, f32[80,2560]{1,0:T(8,128)S(1)}, /*index=5*/f32[80,2560]{1,0:T(8,128)S(1)}) custom-call(bf16[512,2560]{1,0:T(8,128)(2,1)} %attn_hbm.1, bf16[512,2560]{1,0:T(8,128)(2,1)} %og_hbm.1, f32[80,2560]{1,0:T(8,128)} %master_hbm.1, ...), custom_call_target="tpu_custom_call" | custom-call | tf_op jit(solution)/shard_map/pallas_call | solution.py:532
  86.7 2.5 %shard_map.85 = (bf16[512,2560]{1,0:T(8,128)(2,1)}, f32[80,2560]{1,0:T(8,128)}, f32[80,2560]{1,0:T(8,128)}, f32[80,2560]{1,0:T(8,128)}) custom-call(bf16[512,2560]{1,0:T(8,128)(2,1)S(1)} %get-tuple-element.10.ig, f32[80,2560]{1,0:T(8,128)S(1)} %get-tuple-element.11.gw, f32[1,128]{1,0:T(1,128)S(1)} %get-tuple-element.12.sq, ...), custom_call_target="tpu_custom_call" | custom-call | tf_op jit(solution)/shard_map/pallas_call | solution.py:560

commit v5 on v4

--- a/solution.py
+++ b/solution.py
@@ -34,8 +34,9 @@
 def kernel(nb, attn_hbm, og_hbm, master_hbm, m1_hbm, m2_hbm, ig, gw_ref, sq_ref, mst, m1, m2,
            attn_ref, og_ref, rx_og, tbuf, tx, at_own, at_rx, wg, g, rx1, rzb, rx3, fbuf, sqs,
            tz, ty, tl, tsum,
-           l_s, x_s, x_r, p_s, p_r, z_s, z_r, e_s, e_r, c_s, c_r, r_s, r_r, y_s, y_r, f_s, f_r, q_s, q_r,
-           a_s, a_r, b_s, b_r, d_s, d_r, t_s, t_r, u_s, u_r):
+           e_s, e_r, c_s, c_r, q_s, q_r):
+    l_s = x_s = x_r = p_s = p_r = z_s = z_r = r_s = r_r = y_s = y_r = f_s = f_r = None
+    a_s = a_r = b_s = b_r = d_s = d_r = t_s = t_r = u_s = u_r = None
     ns = 4
     nz = nb // 2
     tok, din = attn_ref.shape
@@ -63,31 +64,11 @@
     edge = jnp.logical_or(z == 0, z == nz - 1)
 
     def other(i):
-        f = lax.rem(seq * nb + batch + i, ns * nb)
-        return (f // nb, lax.rem(f, nb))
-
-    lm = pltpu.make_async_copy(master_hbm, mst, l_s.at[2])
-    lm.start()
-    la = pltpu.make_async_copy(attn_hbm, attn_ref, l_s.at[0])
-    la.start()
-    lg = pltpu.make_async_copy(og_hbm, og_ref, l_s.at[1])
-    lg.start()
-    l1 = pltpu.make_async_copy(m1_hbm, m1, l_s.at[3])
-    l1.start()
-    l2 = pltpu.make_async_copy(m2_hbm, m2, l_s.at[4])
-    l2.start()
-    barrier = pltpu.get_barrier_semaphore()
-
-    def greet(s, b):
-        pl.semaphore_signal(barrier, inc=1, device_id=(s, b), device_id_type=MESH)
-
-    greet(sl, batch)
-    greet(sh, batch)
-    greet(*core_dev)
-    for step, ok in ((-2, z > 0), (2, z < nz - 1)):
-        @pl.when(ok)
-        def _():
-            greet(seq, batch + step)
+        b = batch
+        for k in range((nb - 1).bit_length()):
+            if i >> k & 1:
+                b += (1 - batch // 2**k % 2 * 2) * 2**k
+        return (seq, sl, sh, sd)[i // nb], b
 
     near = jnp.minimum(z, nz - 1 - z)
 
@@ -135,8 +116,7 @@
 
     def e_copy(h, i, t):
         v = shard((seq, first[h])[i], zk(t), h)
-        k = (h * 2 + i) * nz + t
-        return remote(v, v, e_s.at[0], e_r.at[k], (last[h], batch))
+        return remote(v, v, e_s.at[0], e_r.at[e_group(t, i)], (last[h], batch))
 
     def c_copy(k, t):
         s, h = ((seq, None), (sl, 0), (sh, 1), (sh, 0), (sd, 0), (sl, 1), (sd, 1))[k]
@@ -266,9 +246,15 @@
         elif h == 1:
             c_copy(0, t).start()
 
-    def ae(t, h, i):
-        e_copy(h, i, t).wait_recv()
-        c_copy(3 + 2 * h + i, t).start()
+    def e_group(t, i):
+        return (0, 0, 1, 2 + i)[t]
+
+    def ae(group):
+        members = [(t, h, i) for t in range(nz) for h in (0, 1) for i in (0, 1) if e_group(t, i) == group]
+        v = wg.at[0, pl.ds(0, len(members) // 2 * r), bcols]
+        all_of(v, e_s.at[0], e_r.at[group]).wait_recv()
+        for t, h, i in members:
+            c_copy(3 + 2 * h + i, t).start()
 
     def rs(j):
         for i in (1, 0):
@@ -337,148 +323,181 @@
     def late(s):
         part(s, zk(nz - 1) * near_cols, block - far_cols)
 
-    xo = remote(og_hbm, rx_og, x_s.at[0], x_r.at[0], core_dev)
-    xt = remote(tx, at_rx, x_s.at[1], x_r.at[1], core_dev)
-
-    lm.wait()
-    wg[seq, wrows(z), :] = mst[...].astype(BF16)
-    pl.semaphore_wait(barrier, 5 - edge.astype(jnp.int32))
-    for k in (0, 1):
-        a_copy(k).start()
-    for h in (0, 1):
-        p_copy(h).start()
-    for h in (0, 1):
-        z_each(h, 0, 0, lambda c: c.start())
-    xo.start()
-    la.wait()
-    for s in range(ns):
-        tbuf[...] = attn_ref[:, s * block:(s + 1) * block].T
-        for zz in range(nz):
-            rows = pl.ds((zz * ns + s) * r, r)
-            at_own[rows, :] = tbuf[pl.ds(pl.multiple_of((zz * 2 + core) * r, 16), r), :]
-            tx[rows, :] = tbuf[pl.ds(pl.multiple_of((zz * 2 + 1 - core) * r, 16), r), :]
-    xt.start()
-    a_copy(0).wait_recv()
-    a_copy(2).start()
-    for h in (1, 0):
-        e_copy(h, 0, 0).start()
-    c_copy(0, 0).start()
-    for h in (0, 1):
-        p_copy(h).wait_recv()
-        z_each(h, 1, 0, lambda c: c.start())
-        e_copy(h, 1, 0).start()
-        c_copy(1 + h, 0).start()
-    for k in (1, 2):
-        a_copy(k).wait_recv()
-    b_each(0, lambda c: c.start())
-    d_copy(0).start()
-    lg.wait()
-    xo.wait_recv()
-    xt.wait_recv()
-
-    def do(on_edge, inside):
-        for ok, events in ((edge, on_edge), (jnp.logical_not(edge), inside)):
-            if events:
-                @pl.when(ok)
-                def _():
-                    for f, *a in events:
-                        f(*a)
-
     hs = (0, 1)
-    ih = [(h, i) for i in (1, 0) for h in hs]
-    grad(0)
-    rs(0)
-    do([(tr, 0)] + [(az, 1, h, 0) for h in hs],
-       [(az, t, h, 0) for h in hs for t in (1, 2)])
-    grad(1)
-    do([(tr, 1), (az, 1, 0, 1)],
-       [(az, t, 0, 1) for t in (1, 2)])
-    grad(2)
-    do([(tr, 2), (az, 1, 1, 1), (rs, 1)],
-       [(az, t, 1, 1) for t in (1, 2)] + [(rs, 1), (rs, 2)])
-    do([(rr, 0, h, i) for h, i in ih[:2]], [])
-    grad(3)
-    do([(rr, 0, h, i) for h, i in ih[2:]] + [(ab, 1)]
-       + [(az, 2, h, 0) for h in hs] + [(rs, 2)] + [(az, 2, h, 1) for h in hs]
-       + [(rr, 1, h, i) for h, i in ih] + [(ab, 2)]
-       + [(ae, t, h, i) for t in (0, 1) for i in hs for h in hs]
-       + [(az, 3, h, i) for i in hs for h in hs]
-       + [(rs, 3)] + [(rr, 2, h, i) for h, i in ih]
-       + [(ae, 2, h, i) for i in hs for h in hs],
-       [(ab, 1), (ab, 2), (tr, 0)]
-       + [e for n, (h, i) in enumerate(ih) for e in ((az, 3, n % 2, n // 2), (rr, 0, h, i))]
-       + [(tr, 1), (tr, 2), (rs, 3)]
-       + [(ae, t, h, i) for t in (0, 1, 2) for i in hs for h in hs]
-       + [(ab, 3)]
-       + [(rr, j, h, i) for h, i in ih[:2] for j in (1, 2)])
-    do([], [(rr, j, h, i) for h, i in ih[2:] for j in (1, 2)])
-    c_wait(0)
-    d_wait(0)
-    early(seq)
-    early(sl)
-    early(sh)
-    early(sd)
-    do([(ab, 3)], [])
-    tl1()
-    for h in hs:
-        ae(3, h, 0)
-    c_wait(1)
-    d_wait(1)
-    late(seq)
-    for h in hs:
-        rl(h, 1)
-    e_copy(0, 1, nz - 1).start()
-    tl2()
-    e_copy(1, 1, nz - 1).start()
-    c_wait(2)
-    late(sl)
-    late(sh)
-    for h in hs:
-        rl(h, 0)
-    for h in hs:
-        f_copy(h).wait_recv()
-        gw_ref[:, rcols[h]] += rx3[h, :, rw[h]].astype(F32)
-    u_copy(1).wait_recv()
-    gw_ref[:, tcols] += tl[...].astype(F32)
-
-    v = gw_ref[...]
-    fold = jnp.sum((v * v).reshape(r // 8, 8, dout), axis=0)
-    acc = fold[:, :128]
-    for i in range(1, dout // 128):
-        acc += fold[:, i * 128:(i + 1) * 128]
-    sqs[0] = jnp.sum(acc, axis=0, keepdims=True)
-
-    def q_copy(i):
-        return remote(sqs.at[0], sqs.at[i], q_s.at[0], q_r.at[0], other(i))
-
-    def q_start(i, carry):
-        q_copy(i).start()
-        return carry
-
-    lax.fori_loop(1, ns * nb, q_start, 0)
-    for h in hs:
-        ae(3, h, 1)
-    xo.wait_send()
-    xt.wait_send()
+
+    def early_scope(*sems):
+        nonlocal l_s, x_s, x_r, p_s, p_r, z_s, z_r, r_s, r_r, y_s, y_r, f_s, f_r
+        nonlocal a_s, a_r, b_s, b_r, d_s, d_r, t_s, t_r, u_s, u_r
+        (l_s, x_s, x_r, p_s, p_r, z_s, z_r, r_s, r_r, y_s, y_r, f_s, f_r,
+         a_s, a_r, b_s, b_r, d_s, d_r, t_s, t_r, u_s, u_r) = sems
+        lm = pltpu.make_async_copy(master_hbm, mst, l_s.at[2])
+        lm.start()
+        la = pltpu.make_async_copy(attn_hbm, attn_ref, l_s.at[0])
+        lg = pltpu.make_async_copy(og_hbm, og_ref, l_s.at[1])
+        l1 = pltpu.make_async_copy(m1_hbm, m1, l_s.at[3])
+        l2 = pltpu.make_async_copy(m2_hbm, m2, l_s.at[4])
+        barrier = pltpu.get_barrier_semaphore()
+
+        def greet(s, b):
+            pl.semaphore_signal(barrier, inc=1, device_id=(s, b), device_id_type=MESH)
+
+        greet(sl, batch)
+        greet(sh, batch)
+        greet(*core_dev)
+        for step, ok in ((-2, z > 0), (2, z < nz - 1)):
+            @pl.when(ok)
+            def _():
+                greet(seq, batch + step)
+
+        xo = remote(og_hbm, rx_og, x_s.at[0], x_r.at[0], core_dev)
+        xt = remote(tx, at_rx, x_s.at[1], x_r.at[1], core_dev)
+
+        lm.wait()
+        la.start()
+        wg[seq, wrows(z), :] = mst[...].astype(BF16)
+        pl.semaphore_wait(barrier, 5 - edge.astype(jnp.int32))
+        for k in (0, 1):
+            a_copy(k).start()
+        for h in (0, 1):
+            p_copy(h).start()
+        for h in (0, 1):
+            z_each(h, 0, 0, lambda c: c.start())
+        xo.start()
+        lg.start()
+        la.wait()
+        for s in range(ns):
+            tbuf[...] = attn_ref[:, s * block:(s + 1) * block].T
+            for zz in range(nz):
+                rows = pl.ds((zz * ns + s) * r, r)
+                at_own[rows, :] = tbuf[pl.ds(pl.multiple_of((zz * 2 + core) * r, 16), r), :]
+                tx[rows, :] = tbuf[pl.ds(pl.multiple_of((zz * 2 + 1 - core) * r, 16), r), :]
+        xt.start()
+        a_copy(0).wait_recv()
+        a_copy(2).start()
+        for h in (1, 0):
+            e_copy(h, 0, 0).start()
+        c_copy(0, 0).start()
+        for h in (0, 1):
+            p_copy(h).wait_recv()
+            z_each(h, 1, 0, lambda c: c.start())
+            e_copy(h, 1, 0).start()
+            c_copy(1 + h, 0).start()
+        for k in (1, 2):
+            a_copy(k).wait_recv()
+        b_each(0, lambda c: c.start())
+        d_copy(0).start()
+        lg.wait()
+        xo.wait_recv()
+        xt.wait_recv()
+
+        def do(on_edge, inside):
+            for ok, events in ((edge, on_edge), (jnp.logical_not(edge), inside)):
+                if events:
+                    @pl.when(ok)
+                    def _():
+                        for f, *a in events:
+                            f(*a)
+
+        ih = [(h, i) for i in (1, 0) for h in hs]
+        grad(0)
+        rs(0)
+        do([(tr, 0)] + [(az, 1, h, 0) for h in hs],
+           [(az, t, h, 0) for h in hs for t in (1, 2)])
+        grad(1)
+        do([(tr, 1), (az, 1, 0, 1)],
+           [(az, t, 0, 1) for t in (1, 2)])
+        grad(2)
+        do([(tr, 2), (az, 1, 1, 1), (rs, 1)],
+           [(az, t, 1, 1) for t in (1, 2)] + [(rs, 1), (rs, 2)])
+        do([(rr, 0, h, i) for h, i in ih[:2]], [])
+        grad(3)
+        do([(rr, 0, h, i) for h, i in ih[2:]] + [(ab, 1)]
+           + [(az, 2, h, 0) for h in hs] + [(rs, 2)] + [(az, 2, h, 1) for h in hs]
+           + [(rr, 1, h, i) for h, i in ih] + [(ab, 2)]
+           + [(ae, 0)]
+           + [(az, 3, h, i) for i in hs for h in hs]
+           + [(rs, 3)] + [(rr, 2, h, i) for h, i in ih]
+           + [(ae, 1)],
+           [(ab, 1), (ab, 2), (tr, 0)]
+           + [e for n, (h, i) in enumerate(ih) for e in ((az, 3, n % 2, n // 2), (rr, 0, h, i))]
+           + [(tr, 1), (tr, 2), (rs, 3)]
+           + [(ae, 0), (ae, 1)]
+           + [(ab, 3)]
+           + [(rr, j, h, i) for h, i in ih[:2] for j in (1, 2)])
+        do([], [(rr, j, h, i) for h, i in ih[2:] for j in (1, 2)])
+        l1.start()
+        l2.start()
+        c_wait(0)
+        d_wait(0)
+        early(seq)
+        early(sl)
+        early(sh)
+        early(sd)
+        do([(ab, 3)], [])
+        tl1()
+        ae(2)
+        c_wait(1)
+        d_wait(1)
+        late(seq)
+        for h in hs:
+            rl(h, 1)
+        e_copy(0, 1, nz - 1).start()
+        tl2()
+        e_copy(1, 1, nz - 1).start()
+        for h in hs:
+            rl(h, 0)
+        for h in hs:
+            f_copy(h).wait_recv()
+        u_copy(1).wait_recv()
+
+        def close(i, acc):
+            rows = pl.ds(pl.multiple_of(i * 16, 16), 16)
+            for c, x in ((rcols[0], rx3[0, rows, rw[0]]), (rcols[1], rx3[1, rows, rw[1]]), (tcols, tl[rows, :])):
+                v = gw_ref[rows, c] + x.astype(F32)
+                gw_ref[rows, c] = v
+                v = v * v
+                for k in range(0, v.shape[1], 128):
+                    acc += v[:8, k:k + 128] + v[8:, k:k + 128]
+            return acc
+
+        acc = lax.fori_loop(0, r // 16, close, jnp.zeros((8, 128), F32))
+        sqs[0] = jnp.sum(acc, axis=0, keepdims=True)
+
+        def q_copy(i):
+            return remote(sqs.at[0], sqs.at[i], q_s.at[0], q_r.at[0], other(i))
+
+        for i in range(ns * nb - 1, 0, -1):
+            q_copy(i).start()
+        c_wait(2)
+        late(sl)
+        late(sh)
+        xo.wait_send()
+        xt.wait_send()
+        for n, sem in ((1, p_s), (1, f_s), (2 * nz, r_s), (2 * (nz - 1), y_s)):
+            all_of(wg.at[0, pl.ds(0, n * r), bcols], sem.at[0], q_r.at[0]).wait_send()
+        for k in range(nz):
+            @pl.when(z == k)
+            def _():
+                for up, n in ((1, k + 1 if k < nz - 1 else 0), (0, nz - k if k else 0)):
+                    if n:
+                        all_of(wg.at[0, pl.ds(0, 2 * n * r), bcols], z_s.at[up], q_r.at[0]).wait_send()
+                        all_of(wg.at[:, pl.ds(0, n * r), tcols], b_s.at[up], q_r.at[0]).wait_send()
+        all_of(wg.at[:, pl.ds(0, nz * r), tcols], d_s.at[0], q_r.at[0]).wait_send()
+        all_of(tz.at[pl.ds(0, nz - 1)], t_s.at[0], q_r.at[0]).wait_send()
+        all_of(wg.at[pl.ds(0, 3), pl.ds(0, r), tcols], a_s.at[0], q_r.at[0]).wait_send()
+        for k in (0, 1):
+            u_copy(k).wait_send()
+        l1.wait()
+        l2.wait()
+
+    sizes = [5, 2, 2, 1, 2, 2, 4 * nz, 1, 4 * nz, 1, 4 * (nz + 1), 1, 2,
+             1, 3, 2, nz, 1, 2, 1, nz + 1, 2, 2]
+    pl.run_scoped(early_scope, *(pltpu.SemaphoreType.DMA((n,)) for n in sizes))
+    ae(3)
     c_wait(3)
     late(sd)
-    for n, sem in ((1, p_s), (1, f_s), (2 * nz, e_s), (2 * nz, r_s), (2 * (nz - 1), y_s)):
-        all_of(wg.at[0, pl.ds(0, n * r), bcols], sem.at[0], q_r.at[0]).wait_send()
-    for k in range(nz):
-        @pl.when(z == k)
-        def _():
-            for up, n in ((1, k + 1 if k < nz - 1 else 0), (0, nz - k if k else 0)):
-                if n:
-                    all_of(wg.at[0, pl.ds(0, 2 * n * r), bcols], z_s.at[up], q_r.at[0]).wait_send()
-                    all_of(wg.at[:, pl.ds(0, n * r), tcols], b_s.at[up], q_r.at[0]).wait_send()
+    all_of(wg.at[0, pl.ds(0, 2 * nz * r), bcols], e_s.at[0], q_r.at[0]).wait_send()
     all_of(wg.at[pl.ds(0, 2), :, bcols], c_s.at[0], q_r.at[0]).wait_send()
-    all_of(wg.at[:, pl.ds(0, nz * r), tcols], d_s.at[0], q_r.at[0]).wait_send()
-    all_of(tz.at[pl.ds(0, nz - 1)], t_s.at[0], q_r.at[0]).wait_send()
-    all_of(wg.at[pl.ds(0, 3), pl.ds(0, r), tcols], a_s.at[0], q_r.at[0]).wait_send()
-    for k in (0, 1):
-        u_copy(k).wait_send()
-    l1.wait()
-    l2.wait()
     all_of(sqs.at[pl.ds(1, ns * nb - 1)], q_s.at[0], q_r.at[0]).wait()
     total = sqs[0]
     for i in range(1, ns * nb):
@@ -526,8 +545,7 @@
     dma = lambda k: pltpu.SemaphoreType.DMA((k,))
     vm = pl.BlockSpec(memory_space=pltpu.VMEM)
     hbm = pl.BlockSpec(memory_space=pl.ANY)
-    sems = [5, 2, 2, 1, 2, 2, 4 * nz, 1, 4 * nz, 1, 4, 1, 4 * nz, 1, 4 * (nz + 1), 1, 2, 1, 1,
-            1, 3, 2, nz, 1, 2, 1, nz + 1, 2, 2]
+    sems = [1, 4, 1, 4, 1, 1]
     flat = (r, dout), F32
     held = pl.pallas_call(
         functools.partial(kernel, nb),

time: 89.6 us -> 88.6 us (0.989)
  Pallas kernels: 88.6 us -> 87.7 us
    pallas_call x1, Pallas kernels: 86.1 us -> 85.1 us  [fused(): pl.pallas_call(functools.partial(kernel, nb), out_shape=tuple((pltpu.VMEM...]
where the time goes in v5:
time: 88.6 us; the launch traced here: 88.3 us
  Pallas kernels  87.7 us (99%)
    pallas_call x1, Pallas kernels, fused(): pl.pallas_call(functools.partial(kernel, nb), out_shape=tuple((pltpu.VMEM...  85.1 us
    pallas_call x1, Pallas kernels, fused(): pl.pallas_call(functools.partial(finish, din * dout), out_shape=(jax.Shap...  2.53 us

profile of v5, /device:TPU:0, one launch (start us, length us, event | category | flops | bytes accessed | tf_op | source)
XLA Modules:
  0.0 88.3 jit_solution(10398880934247242717)
XLA Ops:
  0.6 85.1 %shard_map.84 = (bf16[512,2560]{1,0:T(8,128)(2,1)S(1)}, f32[80,2560]{1,0:T(8,128)S(1)}, f32[1,128]{1,0:T(1,128)S(1)}, f32[80,2560]{1,0:T(8,128)S(1)}, f32[80,2560]{1,0:T(8,128)S(1)}, /*index=5*/f32[80,2560]{1,0:T(8,128)S(1)}) custom-call(bf16[512,2560]{1,0:T(8,128)(2,1)} %attn_hbm.1, bf16[512,2560]{1,0:T(8,128)(2,1)} %og_hbm.1, f32[80,2560]{1,0:T(8,128)} %master_hbm.1, ...), custom_call_target="tpu_custom_call" | custom-call | tf_op jit(solution)/shard_map/pallas_call | solution.py:550
  85.8 2.5 %shard_map.85 = (bf16[512,2560]{1,0:T(8,128)(2,1)}, f32[80,2560]{1,0:T(8,128)}, f32[80,2560]{1,0:T(8,128)}, f32[80,2560]{1,0:T(8,128)}) custom-call(bf16[512,2560]{1,0:T(8,128)(2,1)S(1)} %get-tuple-element.10.ig, f32[80,2560]{1,0:T(8,128)S(1)} %get-tuple-element.11.gw, f32[1,128]{1,0:T(1,128)S(1)} %get-tuple-element.12.sq, ...), custom_call_target="tpu_custom_call" | custom-call | tf_op jit(solution)/shard_map/pallas_call | solution.py:578

commit v6 on v5

--- a/solution.py
+++ b/solution.py
@@ -435,13 +435,13 @@
         early(sd)
         do([(ab, 3)], [])
         tl1()
+        for h in hs:
+            rl(h, 1)
+        e_copy(0, 1, nz - 1).start()
         ae(2)
         c_wait(1)
         d_wait(1)
         late(seq)
-        for h in hs:
-            rl(h, 1)
-        e_copy(0, 1, nz - 1).start()
         tl2()
         e_copy(1, 1, nz - 1).start()
         for h in hs:

time: 88.6 us -> 88.5 us (level)
  no operation moved by 1% of the time
where the time goes in v6:
time: 88.5 us; the launch traced here: 88.3 us
  Pallas kernels  87.7 us (99%)
    pallas_call x1, Pallas kernels, fused(): pl.pallas_call(functools.partial(kernel, nb), out_shape=tuple((pltpu.VMEM...  85.1 us
    pallas_call x1, Pallas kernels, fused(): pl.pallas_call(functools.partial(finish, din * dout), out_shape=(jax.Shap...  2.53 us

profile of v6, /device:TPU:0, one launch (start us, length us, event | category | flops | bytes accessed | tf_op | source)
XLA Modules:
  0.0 88.3 jit_solution(10250479662422044493)
XLA Ops:
  0.6 85.1 %shard_map.84 = (bf16[512,2560]{1,0:T(8,128)(2,1)S(1)}, f32[80,2560]{1,0:T(8,128)S(1)}, f32[1,128]{1,0:T(1,128)S(1)}, f32[80,2560]{1,0:T(8,128)S(1)}, f32[80,2560]{1,0:T(8,128)S(1)}, /*index=5*/f32[80,2560]{1,0:T(8,128)S(1)}) custom-call(bf16[512,2560]{1,0:T(8,128)(2,1)} %attn_hbm.1, bf16[512,2560]{1,0:T(8,128)(2,1)} %og_hbm.1, f32[80,2560]{1,0:T(8,128)} %master_hbm.1, ...), custom_call_target="tpu_custom_call" | custom-call | tf_op jit(solution)/shard_map/pallas_call | solution.py:550
  85.8 2.5 %shard_map.85 = (bf16[512,2560]{1,0:T(8,128)(2,1)}, f32[80,2560]{1,0:T(8,128)}, f32[80,2560]{1,0:T(8,128)}, f32[80,2560]{1,0:T(8,128)}) custom-call(bf16[512,2560]{1,0:T(8,128)(2,1)S(1)} %get-tuple-element.10.ig, f32[80,2560]{1,0:T(8,128)S(1)} %get-tuple-element.11.gw, f32[1,128]{1,0:T(1,128)S(1)} %get-tuple-element.12.sq, ...), custom_call_target="tpu_custom_call" | custom-call | tf_op jit(solution)/shard_map/pallas_call | solution.py:578

commit v7 on v6

--- a/solution.py
+++ b/solution.py
@@ -13,10 +13,14 @@
 BF16 = jnp.bfloat16
 
 
-def update(weight_grad, squares, master, moment_one, moment_two, size):
+def clip_factor(squares, size):
     grad_norm = jnp.sqrt(squares) + 1e-06
     limit = jnp.sqrt(jnp.float32(size))
-    clipped = weight_grad * jnp.minimum(jnp.float32(1.0), limit / grad_norm)
+    return jnp.minimum(jnp.float32(1.0), limit / grad_norm)
+
+
+def update(weight_grad, clip, master, moment_one, moment_two):
+    clipped = weight_grad * clip
     new_one = 0.9 * moment_one + 0.1 * clipped
     new_two = 0.999 * moment_two + 0.001 * clipped * clipped
     first_hat = new_one * (1.0 / (1.0 - 0.9**STEP))
@@ -508,18 +512,18 @@
 def finish(size, ig, gw, sq, mst, m1, m2, ig_hbm, nm_hbm, n1_hbm, n2_hbm, nm, n1, n2, i_s, o_s):
     ci = pltpu.make_async_copy(ig, ig_hbm, i_s.at[0])
     ci.start()
-    steps = gw.shape[0] // 8
-    squares = jnp.sum(sq[...], axis=1, keepdims=True)
+    steps = gw.shape[0] // 16
+    clip = clip_factor(jnp.sum(sq[...], axis=1, keepdims=True), size)
 
     def copies(i):
-        rows = pl.ds(pl.multiple_of(i * 8, 8), 8)
+        rows = pl.ds(pl.multiple_of(i * 16, 16), 16)
         return [pltpu.make_async_copy(a.at[rows], b.at[rows], o_s.at[k, i])
                 for k, (a, b) in enumerate(((nm, nm_hbm), (n1, n1_hbm), (n2, n2_hbm)))]
 
     def body(i, carry):
-        rows = pl.ds(pl.multiple_of(i * 8, 8), 8)
+        rows = pl.ds(pl.multiple_of(i * 16, 16), 16)
         nm[rows, :], n1[rows, :], n2[rows, :] = update(
-            gw[rows, :], squares, mst[rows, :], m1[rows, :], m2[rows, :], size)
+            gw[rows, :], clip, mst[rows, :], m1[rows, :], m2[rows, :])
         for c in copies(i):
             c.start()
         return carry
@@ -580,7 +584,7 @@
         out_shape=(jax.ShapeDtypeStruct((tok, din), BF16),) + (jax.ShapeDtypeStruct(*flat),) * 3,
         in_specs=[vm] * 6,
         out_specs=(hbm,) * 4,
-        scratch_shapes=[pltpu.VMEM(*flat)] * 3 + [dma(1), pltpu.SemaphoreType.DMA((3, r // 8))],
+        scratch_shapes=[pltpu.VMEM(*flat)] * 3 + [dma(1), pltpu.SemaphoreType.DMA((3, r // 16))],
         compiler_params=pltpu.CompilerParams(vmem_limit_bytes=6_000_000),
     )(*(pltpu.with_memory_space_constraint(v, pltpu.VMEM) for v in held))
 
@@ -611,7 +615,8 @@
     if ns == 4 and nb == 8 and r % 16 == 0 and (nb * r) % 128 == 0 and dout % 256 == 0:
         return fused(attn_out, out_grad, master, moment_one, moment_two, ns, nb)
     input_grad, weight_grad, squares = plain(attn_out, out_grad, master.astype(BF16))
-    return (input_grad,) + update(weight_grad, squares, master, moment_one, moment_two, din * dout)
+    return (input_grad,) + update(
+        weight_grad, clip_factor(squares, din * dout), master, moment_one, moment_two)
 
 
 def solution(mesh):

time: 88.5 us -> 88.3 us (level)
  no operation moved by 1% of the time
where the time goes in v7:
time: 88.3 us; the launch traced here: 88.2 us
  Pallas kernels  87.5 us (99%)
    pallas_call x1, Pallas kernels, fused(): pl.pallas_call(functools.partial(kernel, nb), out_shape=tuple((pltpu.VMEM...  85.1 us
    pallas_call x1, Pallas kernels, fused(): pl.pallas_call(functools.partial(finish, din * dout), out_shape=(jax.Shap...  2.41 us

profile of v7, /device:TPU:0, one launch (start us, length us, event | category | flops | bytes accessed | tf_op | source)
XLA Modules:
  0.0 88.2 jit_solution(2972012786120441105)
XLA Ops:
  0.6 85.1 %shard_map.84 = (bf16[512,2560]{1,0:T(8,128)(2,1)S(1)}, f32[80,2560]{1,0:T(8,128)S(1)}, f32[1,128]{1,0:T(1,128)S(1)}, f32[80,2560]{1,0:T(8,128)S(1)}, f32[80,2560]{1,0:T(8,128)S(1)}, /*index=5*/f32[80,2560]{1,0:T(8,128)S(1)}) custom-call(bf16[512,2560]{1,0:T(8,128)(2,1)} %attn_hbm.1, bf16[512,2560]{1,0:T(8,128)(2,1)} %og_hbm.1, f32[80,2560]{1,0:T(8,128)} %master_hbm.1, ...), custom_call_target="tpu_custom_call" | custom-call | tf_op jit(solution)/shard_map/pallas_call | solution.py:554
  85.8 2.4 %shard_map.85 = (bf16[512,2560]{1,0:T(8,128)(2,1)}, f32[80,2560]{1,0:T(8,128)}, f32[80,2560]{1,0:T(8,128)}, f32[80,2560]{1,0:T(8,128)}) custom-call(bf16[512,2560]{1,0:T(8,128)(2,1)S(1)} %get-tuple-element.10.ig, f32[80,2560]{1,0:T(8,128)S(1)} %get-tuple-element.11.gw, f32[1,128]{1,0:T(1,128)S(1)} %get-tuple-element.12.sq, ...), custom_call_target="tpu_custom_call" | custom-call | tf_op jit(solution)/shard_map/pallas_call | solution.py:582

commit v8 on v7

--- a/solution.py
+++ b/solution.py
@@ -437,17 +437,17 @@
         early(sl)
         early(sh)
         early(sd)
+        tl1()
         do([(ab, 3)], [])
-        tl1()
         for h in hs:
             rl(h, 1)
         e_copy(0, 1, nz - 1).start()
         ae(2)
+        tl2()
+        e_copy(1, 1, nz - 1).start()
         c_wait(1)
         d_wait(1)
         late(seq)
-        tl2()
-        e_copy(1, 1, nz - 1).start()
         for h in hs:
             rl(h, 0)
         for h in hs:

time: 88.3 us -> 88.3 us (level)
  no operation moved by 1% of the time
where the time goes in v8:
time: 88.3 us; the launch traced here: 88.2 us
  Pallas kernels  87.5 us (99%)
    pallas_call x1, Pallas kernels, fused(): pl.pallas_call(functools.partial(kernel, nb), out_shape=tuple((pltpu.VMEM...  85.1 us
    pallas_call x1, Pallas kernels, fused(): pl.pallas_call(functools.partial(finish, din * dout), out_shape=(jax.Shap...  2.41 us

profile of v8, /device:TPU:0, one launch (start us, length us, event | category | flops | bytes accessed | tf_op | source)
XLA Modules:
  0.0 88.2 jit_solution(15042909701993645811)
XLA Ops:
  0.6 85.1 %shard_map.84 = (bf16[512,2560]{1,0:T(8,128)(2,1)S(1)}, f32[80,2560]{1,0:T(8,128)S(1)}, f32[1,128]{1,0:T(1,128)S(1)}, f32[80,2560]{1,0:T(8,128)S(1)}, f32[80,2560]{1,0:T(8,128)S(1)}, /*index=5*/f32[80,2560]{1,0:T(8,128)S(1)}) custom-call(bf16[512,2560]{1,0:T(8,128)(2,1)} %attn_hbm.1, bf16[512,2560]{1,0:T(8,128)(2,1)} %og_hbm.1, f32[80,2560]{1,0:T(8,128)} %master_hbm.1, ...), custom_call_target="tpu_custom_call" | custom-call | tf_op jit(solution)/shard_map/pallas_call | solution.py:554
  85.8 2.4 %shard_map.85 = (bf16[512,2560]{1,0:T(8,128)(2,1)}, f32[80,2560]{1,0:T(8,128)}, f32[80,2560]{1,0:T(8,128)}, f32[80,2560]{1,0:T(8,128)}) custom-call(bf16[512,2560]{1,0:T(8,128)(2,1)S(1)} %get-tuple-element.10.ig, f32[80,2560]{1,0:T(8,128)S(1)} %get-tuple-element.11.gw, f32[1,128]{1,0:T(1,128)S(1)} %get-tuple-element.12.sq, ...), custom_call_target="tpu_custom_call" | custom-call | tf_op jit(solution)/shard_map/pallas_call | solution.py:582
